TPU v7x, 512 devices: a whole 4x8x8 slice. The times are simulated.
512 devices in a mesh: dp: 8 (over x, core), expert: 64 (over y, z).
Axes of the slice: x: 4, y: 8, z: 8, core: 2. Of those that a mesh axis runs over, the one named last changes fastest.
Arguments:
- q_latent: bfloat16 [2048, 16, 576], P(('expert', 'dp')), may hold values from -48 to 48
- latent_cache: bfloat16 [2048, 512, 576], P(('expert', 'dp')), may hold values from -10 to 10
- lengths: int32 [2048], P(('expert', 'dp')), may hold values from 2 to 512
- residual: bfloat16 [2048, 2048], P(('expert', 'dp')), may hold values from -6 to 6
- adapter_ids: int32 [2048], P(('expert', 'dp')), may hold values from 0 to 127
- value_out: bfloat16 [8192, 2048], P('expert'), may hold values from -0.0625 to 0.0625
- adapter_down: bfloat16 [8192, 2048], P('expert'), may hold values from -0.0625 to 0.0625
- adapter_up_factors: bfloat16 [2048, 2048], P('expert'), may hold values from -1.5 to 1.5
- norm_gain: bfloat16 [2048], replicated, may hold values from 0.099609375 to 1.8984375
- expert_ids: int32 [2048, 6], P('expert'), may hold values from 0 to 63, all different within a row; in each aligned block of 32 rows (0 to 31, 32 to 63, ...) at most 8 rows name the same one
- gate_weights: float32 [2048, 6], P('expert'), may hold values from 0.05 to 0.5
- w_gate: bfloat16 [64, 2048, 1024], P('expert', None, 'dp'), may hold values from -0.125 to 0.125
- w_up: bfloat16 [64, 2048, 1024], P('expert', None, 'dp'), may hold values from -0.125 to 0.125
- w_down: bfloat16 [64, 2048, 1024], P('expert', None, 'dp'), may hold values from -0.1875 to 0.1875
Outputs:
- layer_out: bfloat16 [2048, 2048], P(('expert', 'dp'))
Inputs may be any that keep to these rules, and one draw needn't show every extreme that they name: `expert_ids`: each row names 6 different experts. Requests e * 32 to e * 32 + 31 form aligned blocks; in each block no expert is named by more than 8 rows, and in some block an expert is named by exactly 8 rows.
All inputs are finite; a program needn't handle non-finite values.
Results may differ from a plain program's by a relative error of at most 0.008.
Values may be sent and summed in bfloat16 or wider, within the bound.
No kernel may reach another device: no remote copies, remote signals or barrier semaphores. Data moves between devices by JAX's collectives and lax.ppermute only.
A program may use at most 64 MiB of HBM per device.

v0:
```python
import functools

import jax
import jax.numpy as jnp
from jax import lax
from jax.sharding import Mesh
from jax.sharding import PartitionSpec as P

LAT = 512
ADAPTER_RANK = 16
EXPERT = ("expert_0", "expert_1")
EXPERT_DP = ("expert_0", "expert_1", "dp")


SOFTMAX_SCALE = 192.0 ** (-0.5)
ADAPTER_SCALE = 2.0
EPSILON = 1e-06


def copy_for_each(shard, axis):
    copies = jnp.broadcast_to(shard, (lax.axis_size(axis), *shard.shape))
    return lax.all_to_all(copies, axis, split_axis=0, concat_axis=0, tiled=True)


def joined_along(blocks, dim):
    dims = list(blocks.shape[1:])
    dims[dim] *= blocks.shape[0]
    return jnp.moveaxis(blocks, 0, dim).reshape(dims)


def gathered_copies(shard, axis, dim):
    blocks = copy_for_each(shard, axis)
    return joined_along(blocks, dim)


def one_axis_at_a_time(shard, axes):
    return functools.reduce(lax.psum, axes, shard)


def cut_along(shard, dim, count):
    dims = shard.shape
    blocks = shard.reshape(*dims[:dim], count, dims[dim] // count, *dims[dim + 1 :])
    return jnp.moveaxis(blocks, dim, 0)


def sum_at_owner(shard, axis, dim):
    blocks = cut_along(shard, dim, lax.axis_size(axis))
    arrived = lax.all_to_all(blocks, axis, split_axis=0, concat_axis=0, tiled=True)
    return arrived.sum(axis=0)


def in_one_piece(arrays, axis, dim, along):
    both = jnp.concatenate(arrays, axis=along)
    whole, at, gathered = (lax.all_gather(both, axis, axis=dim, tiled=True), 0, [])
    for a in arrays:
        gathered.append(lax.slice_in_dim(whole, at, at + a.shape[along], axis=along))
        at += a.shape[along]
    return tuple(gathered)


def summed_on_arrival(shard, axis, dim):
    blocks = cut_along(shard, dim, lax.axis_size(axis))
    arrived = lax.all_to_all(blocks, axis, split_axis=0, concat_axis=0, tiled=True)
    return arrived.astype(jnp.float32).sum(axis=0)


def attend_one(query, latent_rows, length):
    scores = (
        lax.dot_general(
            query, latent_rows, (((1,), (1,)), ((), ())), preferred_element_type=jnp.float32
        )
        * SOFTMAX_SCALE
    )
    valid_mask = jnp.arange(latent_rows.shape[0], dtype=jnp.int32) < length
    scores = jnp.where(valid_mask[None, :], scores, -1e30)
    row_max = jnp.max(scores, axis=1, keepdims=True)
    raised = jnp.exp(scores - row_max)
    weights_bf = (raised / jnp.sum(raised, axis=1, keepdims=True)).astype(jnp.bfloat16)
    return jnp.dot(weights_bf, latent_rows[:, :LAT], preferred_element_type=jnp.float32).astype(
        jnp.bfloat16
    )


def expert_rows(tokens, gate_part, up_part, down_part):
    gate_act = jnp.dot(tokens, gate_part, preferred_element_type=jnp.float32)
    up_act = jnp.dot(tokens, up_part, preferred_element_type=jnp.float32)
    hidden_bf = (jax.nn.silu(gate_act) * up_act).astype(jnp.bfloat16)
    return lax.dot_general(
        hidden_bf, down_part, (((1,), (1,)), ((), ())), preferred_element_type=jnp.float32
    )


def local(
    q_latent,
    latent_cache,
    lengths,
    residual,
    adapter_ids,
    value_out,
    adapter_down,
    adapter_up_factors,
    norm_gain,
    expert_ids,
    gate_weights,
    w_gate,
    w_up,
    w_down,
):
    requests = residual.shape[0]
    model_width = residual.shape[1]
    head_count = q_latent.shape[1]
    latent_out = jax.vmap(attend_one)(q_latent, latent_cache, lengths).reshape(
        requests, head_count * LAT
    )
    pieces = lax.all_to_all(latent_out, EXPERT, split_axis=1, concat_axis=0, tiled=True)
    group_ids = gathered_copies(adapter_ids, EXPERT, 0)
    group_rows = pieces.shape[0]
    adapters = adapter_down.shape[1] // ADAPTER_RANK
    owned_count = adapter_up_factors.shape[0] // ADAPTER_RANK
    down_projected_rows = jnp.dot(pieces, adapter_down, preferred_element_type=jnp.float32).reshape(
        group_rows, adapters, ADAPTER_RANK
    )
    chosen_adapters = group_ids[:, None] == jnp.arange(adapters, dtype=jnp.int32)[None, :]
    adapter_output = jnp.sum(
        jnp.where(chosen_adapters[:, :, None], down_projected_rows, 0.0), axis=1
    )
    adapter_down_rows = one_axis_at_a_time(adapter_output, EXPERT)
    adapter_scaled_output = (ADAPTER_SCALE * adapter_down_rows).astype(jnp.bfloat16)
    first_owned = lax.axis_index(EXPERT) * owned_count
    holder_mask = (
        group_ids[:, None] == first_owned + jnp.arange(owned_count, dtype=jnp.int32)[None, :]
    )
    spread_rows = jnp.where(
        holder_mask[:, :, None], adapter_scaled_output[:, None, :], jnp.zeros((), jnp.bfloat16)
    ).reshape(group_rows, owned_count * ADAPTER_RANK)
    attention = sum_at_owner(
        jnp.dot(pieces, value_out, preferred_element_type=jnp.float32)
        + jnp.dot(spread_rows, adapter_up_factors, preferred_element_type=jnp.float32),
        EXPERT,
        0,
    )
    residual_flow = residual.astype(jnp.float32) + attention
    inverse_rms = lax.rsqrt(
        jnp.mean(residual_flow * residual_flow, axis=1, keepdims=True) + EPSILON
    )
    normed = (residual_flow * inverse_rms * norm_gain.astype(jnp.float32)).astype(jnp.bfloat16)
    column = gathered_copies(normed, "dp", 0)
    tokens = column.shape[0]
    top_count = expert_ids.shape[1]
    experts = lax.axis_size(EXPERT) * w_gate.shape[0]
    share_size = max(1, 2 * requests * top_count // experts)
    dp_count = lax.axis_size("dp")
    slot_count = share_size * dp_count
    position = lax.axis_index("dp")
    member = expert_ids[:, :, None] == jnp.arange(experts, dtype=jnp.int32)[None, None, :]
    flat_hits = member.reshape(tokens * top_count, experts).astype(jnp.int32)
    slot_rank = jnp.sum((jnp.cumsum(flat_hits, axis=0) - 1) * flat_hits, axis=1).reshape(
        tokens, top_count
    )
    placed = member[:, :, :, None] & (
        slot_rank[:, :, None, None] == jnp.arange(slot_count, dtype=jnp.int32)[None, None, None, :]
    )
    routing = jnp.any(placed, axis=1).reshape(tokens, experts * slot_count)
    combine = jnp.sum(jnp.where(placed, gate_weights[:, :, None, None], 0.0), axis=1).reshape(
        tokens, experts * slot_count
    )
    routing_rows = routing.T.astype(jnp.bfloat16)
    portion = lax.dynamic_slice_in_dim(
        routing_rows.reshape(experts, slot_count, tokens), position * share_size, share_size, 1
    ).reshape(experts * share_size, tokens)
    outgoing = (
        jnp.dot(portion, column, preferred_element_type=jnp.float32)
        .astype(jnp.bfloat16)
        .reshape(experts, share_size, model_width)
    )
    own_share = lax.all_to_all(outgoing, EXPERT, split_axis=0, concat_axis=0, tiled=True)
    weights_share = lax.dynamic_slice_in_dim(
        combine.reshape(tokens, experts, slot_count), position * share_size, share_size, 2
    ).reshape(tokens, experts * share_size)
    share_rows = own_share.reshape(experts * share_size, model_width)
    pieces_now = in_one_piece((w_gate, w_up, w_down), "dp", 2, 0)
    result = expert_rows(share_rows, pieces_now[0][0], pieces_now[1][0], pieces_now[2][0])
    returned = lax.all_to_all(
        result.reshape(experts, share_size, model_width).astype(jnp.bfloat16),
        EXPERT,
        split_axis=0,
        concat_axis=0,
        tiled=True,
    ).astype(jnp.float32)
    routed_column = jnp.dot(
        weights_share,
        returned.reshape(experts * share_size, model_width),
        precision=lax.Precision.HIGHEST,
        preferred_element_type=jnp.float32,
    )
    routed_sum = summed_on_arrival(routed_column.astype(jnp.bfloat16), "dp", 0)
    return (residual_flow + routed_sum).astype(jnp.bfloat16)


def solution(mesh):
    split = Mesh(mesh.devices.reshape(mesh.shape["dp"], 8, 8), ("dp", "expert_0", "expert_1"))
    in_specs = (
        P(EXPERT_DP, None, None),
        P(EXPERT_DP, None, None),
        P(EXPERT_DP),
        P(EXPERT_DP, None),
        P(EXPERT_DP),
        P(EXPERT, None),
        P(EXPERT, None),
        P(EXPERT, None),
        P(),
        P(EXPERT, None),
        P(EXPERT, None),
        P(EXPERT, None, "dp"),
        P(EXPERT, None, "dp"),
        P(EXPERT, None, "dp"),
    )
    out_specs = P(EXPERT_DP, None)
    return jax.shard_map(local, mesh=split, in_specs=in_specs, out_specs=out_specs, check_vma=False)
```

profile of v0, /device:TPU:1, one launch (start us, length us, event | category | flops | bytes accessed | tf_op | source)
XLA Modules:
  0.0 246.6 jit_solution(12771634522854351445)
XLA Ops:
  6.5 0.0 all-gather.2.cloned.1.call-start
  6.6 2.9 %pad_maximum_fusion = bf16[3,2048,128]{2,1,0:T(8,128)(2,1)} fusion(bf16[1,2048,128]{2,1,0:T(8,128)(2,1)} %param.27, bf16[1,2048,128]{2,1,0:T(8,128)(2,1)} %param.26, bf16[1,2048,128]{2,1,0:T(8,128)(2,1)} %param.25), kind=kLoop, calls=%fused_computation.16 | loop fusion | flops 1572864 | bytes 3145728 | tf_op jit(solution)/shard_map/concatenate | solution.py:53
  9.5 0.6 broadcast_in_dim.81
  10.1 17.4 %all-to-all-start.1 = ((s32[64,1,4]{2,1,0:T(1,128)}), s32[64,1,4]{2,1,0:T(1,128)}, u32[]{:S(2)}, u32[]{:S(2)}) async-start(s32[64,1,4]{2,1,0:T(1,128)} %broadcast_in_dim.81), calls=%async_computation.1 | async-start | bytes 65536 | tf_op jit(solution)/shard_map/all_to_all | solution.py:22
  27.5 0.1 iota_compare_fusion.5
  27.6 1.4 fusion.12
  29.0 0.2 fusion.39
  29.2 1.3 fusion.14
  30.5 0.9 all_to_all.33
  31.4 0.7 copy.55
  32.1 0.3 copy.56
  32.3 5.9 %all-to-all-done.1 = s32[64,1,4]{2,1,0:T(1,128)} async-done(((s32[64,1,4]{2,1,0:T(1,128)}), s32[64,1,4]{2,1,0:T(1,128)}, u32[]{:S(2)}, u32[]{:S(2)}) %all-to-all-start.1) | async-done | bytes 1056 | tf_op jit(solution)/shard_map/all_to_all | solution.py:22
  38.2 6.2 %all-to-all-start = ((bf16[4,64,128]{2,0,1:T(4,128)(2,1)}), bf16[4,64,128]{2,0,1:T(4,128)(2,1)S(1)}, u32[]{:S(2)}, u32[]{:S(2)}) async-start(bf16[4,64,128]{2,0,1:T(4,128)(2,1)} %copy.55), calls=%async_computation | async-start | bytes 131072 | tf_op jit(solution)/shard_map/all_to_all | solution.py:115
  44.4 0.5 broadcast.121
  44.9 1.5 reduce.5
  46.4 0.1 eq.89
  46.6 0.1 broadcast_compare_fusion
  46.6 8.9 %all-to-all-done = bf16[4,64,128]{2,0,1:T(4,128)(2,1)S(1)} async-done(((bf16[4,64,128]{2,0,1:T(4,128)(2,1)}), bf16[4,64,128]{2,0,1:T(4,128)(2,1)S(1)}, u32[]{:S(2)}, u32[]{:S(2)}) %all-to-all-start) | async-done | bytes 65568 | tf_op jit(solution)/shard_map/all_to_all | solution.py:115
  55.5 0.5 select_reduce_fusion
  56.0 23.1 %psum.14 = f32[256,16]{0,1:T(8,128)S(1)} all-reduce(f32[256,16]{0,1:T(8,128)S(1)} %select_reduce_fusion), channel_id=1, replica_groups=mesh['dp'=8,'expert_0'=8,'expert_1'=8] {'expert_0'}, use_global_device_ids=true, to_apply=%region_3.4 | all-reduce | flops 4096 | bytes 32768 | tf_op jit(solution)/shard_map/psum | solution.py:37
  79.1 21.6 %psum.15 = f32[256,16]{0,1:T(8,128)S(1)} all-reduce(f32[256,16]{0,1:T(8,128)S(1)} %psum.14), channel_id=1, replica_groups=mesh['dp'=8,'expert_0'=8,'expert_1'=8] {'expert_1'}, use_global_device_ids=true, to_apply=%region_4.5 | all-reduce | flops 4096 | bytes 32768 | tf_op jit(solution)/shard_map/psum | solution.py:37
  100.7 0.4 fusion.40
  101.2 0.5 convolution_add_fusion
  101.6 1.7 reshape.163
  103.3 7.5 %all-to-all-start.2 = ((f32[64,4,2048]{2,1,0:T(4,128)}), f32[64,4,2048]{2,1,0:T(4,128)S(1)}, u32[]{:S(2)}, u32[]{:S(2)}) async-start(f32[64,4,2048]{2,1,0:T(4,128)} %reshape.163), calls=%async_computation.2 | async-start | bytes 4194304 | tf_op jit(solution)/shard_map/all_to_all | solution.py:48
  110.9 0.1 copy.58
  111.0 0.1 eq.99
  111.1 0.6 reduce-window.6
  111.7 0.2 slice_reduce_fusion
  112.0 0.1 bitcast_bitcast_fusion
  112.1 0.1 eq.106
  112.2 0.1 iota_compare_fusion.1
  112.3 0.1 iota_compare_fusion
  112.4 37.7 %all-to-all-done.2 = f32[64,4,2048]{2,1,0:T(4,128)S(1)} async-done(((f32[64,4,2048]{2,1,0:T(4,128)}), f32[64,4,2048]{2,1,0:T(4,128)S(1)}, u32[]{:S(2)}, u32[]{:S(2)}) %all-to-all-start.2) | async-done | bytes 2097184 | tf_op jit(solution)/shard_map/all_to_all | solution.py:48
  150.1 0.4 reduce_sum.65
  150.5 0.1 multiply_reduce_fusion
  150.6 0.1 multiply_convert_fusion
  150.7 0.7 broadcast_in_dim.89
  151.4 17.3 %all-to-all-start.3 = ((bf16[8,4,2048]{2,1,0:T(4,128)(2,1)}), bf16[8,4,2048]{2,1,0:T(4,128)(2,1)S(1)}, u32[]{:S(2)}, u32[]{:S(2)}) async-start(bf16[8,4,2048]{2,1,0:T(4,128)(2,1)} %broadcast_in_dim.89), calls=%async_computation.3 | async-start | bytes 262144 | tf_op jit(solution)/shard_map/all_to_all | solution.py:22
  168.7 0.3 and_reduce_fusion
  169.0 0.2 copy.63
  169.2 0.1 constant_dynamic-slice_fusion
  169.3 0.1 copy.64
  169.3 4.6 %all-to-all-done.3 = bf16[8,4,2048]{2,1,0:T(4,128)(2,1)S(1)} async-done(((bf16[8,4,2048]{2,1,0:T(4,128)(2,1)}), bf16[8,4,2048]{2,1,0:T(4,128)(2,1)S(1)}, u32[]{:S(2)}, u32[]{:S(2)}) %all-to-all-start.3) | async-done | bytes 131104 | tf_op jit(solution)/shard_map/all_to_all | solution.py:22
  174.0 0.3 fusion.6
  174.3 0.5 broadcast.123
  174.8 0.8 reduce.6
  175.6 0.2 reshape.187
  175.7 22.4 %all_to_all.50 = bf16[64,2,1024]{2,1,0:T(2,128)(2,1)S(1)} all-to-all(bf16[64,2,1024]{2,1,0:T(2,128)(2,1)S(1)} %reshape.187), channel_id=1, replica_groups=mesh['dp'=8,'expert_0'=8,'expert_1'=8] {'expert_0','expert_1'}, dimensions={0} | all-to-all | bytes 524288 | tf_op jit(solution)/shard_map/all_to_all | solution.py:176
  198.1 0.2 reshape.188
  198.4 3.1 %fusion.3 = f32[64,1024]{1,0:T(8,128)S(1)} fusion(bf16[3,2048,1024]{2,1,0:T(8,128)(2,1)} %all-gather.2.cloned.1.call-done, bf16[64,1,2048]{2,1,0:T(2,128)(2,1)S(1)} %reshape.188), kind=kOutput, calls=%fused_computation.6 | convolution fusion | flops 268435456 | bytes 4718592 | tf_op jit(solution)/shard_map/dot_general | solution.py:85
  201.4 5.6 %fusion.5 = bf16[64,1,2048]{2,0,1:T(8,128)(2,1)S(1)} fusion(bf16[3,2048,1024]{2,1,0:T(8,128)(2,1)} %all-gather.2.cloned.1.call-done, f32[64,1024]{1,0:T(8,128)S(1)} %fusion.3, bf16[64,1,2048]{2,1,0:T(2,128)(2,1)S(1)} %reshape.188), kind=kOutput, calls=%fused_computation.10 | convolution fusion | flops 537395200 | bytes 9175040 | tf_op jit(solution)/shard_map/dot_general | solution.py:88
  207.1 0.8 reduce.7
  207.9 0.9 reshape.189
  208.7 6.0 %all-to-all-start.5 = ((bf16[64,2,1024]{2,1,0:T(2,128)(2,1)}), bf16[64,2,1024]{2,1,0:T(2,128)(2,1)S(1)}, u32[]{:S(2)}, u32[]{:S(2)}) async-start(bf16[64,2,1024]{2,1,0:T(2,128)(2,1)} %reshape.189), calls=%async_computation.5 | async-start | bytes 524288 | tf_op jit(solution)/shard_map/all_to_all | solution.py:183
  214.7 0.1 copy.62
  214.8 0.6 fusion.17
  215.4 11.8 %all-to-all-done.5 = bf16[64,2,1024]{2,1,0:T(2,128)(2,1)S(1)} async-done(((bf16[64,2,1024]{2,1,0:T(2,128)(2,1)}), bf16[64,2,1024]{2,1,0:T(2,128)(2,1)S(1)}, u32[]{:S(2)}, u32[]{:S(2)}) %all-to-all-start.5) | async-done | bytes 262176 | tf_op jit(solution)/shard_map/all_to_all | solution.py:183
  227.2 0.2 reshape.190
  227.4 0.4 convolution_convert_fusion.1
  227.8 0.1 reshape.174
  227.8 11.2 %all_to_all.51 = bf16[8,4,2048]{2,1,0:T(4,128)(2,1)S(1)} all-to-all(bf16[8,4,2048]{2,1,0:T(4,128)(2,1)S(1)} %reshape.174), channel_id=1, replica_groups=mesh['dp'=8,'expert_0'=8,'expert_1'=8] {'dp'}, dimensions={0} | all-to-all | bytes 262144 | tf_op jit(solution)/shard_map/all_to_all | solution.py:63
  239.1 0.1 convert_reduce_fusion
  239.1 0.6 add_convert_fusion
  (35 shorter events, 0.3 us)
Async XLA Ops:
  6.5 94.2 %copy-start = (bf16[128,2048]{1,0:T(8,128)(2,1)S(1)}, bf16[128,2048]{1,0:T(8,128)(2,1)}, u32[]{:S(2)}) copy-start(bf16[128,2048]{1,0:T(8,128)(2,1)} %param.19) | copy-start | bytes 1572868
  6.5 2.9 %copy-start.8 = (s32[4]{0:T(128)S(1)}, s32[4]{0:T(128)}, u32[]{:S(2)}) copy-start(s32[4]{0:T(128)} %param.18) | copy-start | bytes 52
  6.5 21.0 %copy-start.9 = (s32[4]{0:T(128)S(1)}, s32[4]{0:T(128)}, u32[]{:S(2)}) copy-start(s32[4]{0:T(128)} %param.16) | copy-start | bytes 52
  6.5 21.0 %copy-start.1 = (bf16[4,512,576]{1,2,0:T(8,128)(2,1)S(1)}, bf16[4,512,576]{1,2,0:T(8,128)(2,1)}, u32[]{:S(2)}) copy-start(bf16[4,512,576]{1,2,0:T(8,128)(2,1)} %param.15) | copy-start | bytes 7077892
  6.5 191.8 %all-gather.2.cloned.1.call-start = ((), (), s32[]{:S(2)}) async-start(), calls=%async_computation.7 | async-start | bytes 14155776 | tf_op jit(solution)/shard_map/all_gather | solution.py:54
  10.1 28.1 %all-to-all-start.1 = ((s32[64,1,4]{2,1,0:T(1,128)}), s32[64,1,4]{2,1,0:T(1,128)}, u32[]{:S(2)}, u32[]{:S(2)}) async-start(s32[64,1,4]{2,1,0:T(1,128)} %broadcast_in_dim.81), calls=%async_computation.1 | async-start | bytes 65536 | tf_op jit(solution)/shard_map/all_to_all | solution.py:22
  27.6 4.5 %copy-start.2 = (bf16[128,2048]{1,0:T(8,128)(2,1)S(1)}, bf16[128,2048]{1,0:T(8,128)(2,1)}, u32[]{:S(2)}) copy-start(bf16[128,2048]{1,0:T(8,128)(2,1)} %param.20) | copy-start | bytes 1572868
  38.2 17.3 %all-to-all-start = ((bf16[4,64,128]{2,0,1:T(4,128)(2,1)}), bf16[4,64,128]{2,0,1:T(4,128)(2,1)S(1)}, u32[]{:S(2)}, u32[]{:S(2)}) async-start(bf16[4,64,128]{2,0,1:T(4,128)(2,1)} %copy.55), calls=%async_computation | async-start | bytes 131072 | tf_op jit(solution)/shard_map/all_to_all | solution.py:115
  55.5 45.7 %copy-start.4 = (bf16[32,2048]{1,0:T(8,128)(2,1)S(1)}, bf16[32,2048]{1,0:T(8,128)(2,1)}, u32[]{:S(2)}) copy-start(bf16[32,2048]{1,0:T(8,128)(2,1)} %param.21) | copy-start | bytes 393220
  103.3 7.5 %copy-start.5 = (bf16[2048]{0:T(1024)(128)(2,1)S(1)}, bf16[2048]{0:T(1024)(128)(2,1)}, u32[]{:S(2)}) copy-start(bf16[2048]{0:T(1024)(128)(2,1)} %param.22) | copy-start | bytes 12292
  103.3 7.6 %copy-start.6 = (s32[32,6]{0,1:T(8,128)S(1)}, s32[32,6]{0,1:T(8,128)}, u32[]{:S(2)}) copy-start(s32[32,6]{0,1:T(8,128)} %param.23) | copy-start | bytes 2308
  103.3 46.8 %all-to-all-start.2 = ((f32[64,4,2048]{2,1,0:T(4,128)}), f32[64,4,2048]{2,1,0:T(4,128)S(1)}, u32[]{:S(2)}, u32[]{:S(2)}) async-start(f32[64,4,2048]{2,1,0:T(4,128)} %reshape.163), calls=%async_computation.2 | async-start | bytes 4194304 | tf_op jit(solution)/shard_map/all_to_all | solution.py:48
  110.9 39.6 %copy-start.3 = (bf16[4,2048]{1,0:T(4,128)(2,1)S(1)}, bf16[4,2048]{1,0:T(4,128)(2,1)}, u32[]{:S(2)}) copy-start(bf16[4,2048]{1,0:T(4,128)(2,1)} %param.17) | copy-start | bytes 49156
  151.4 22.6 %all-to-all-start.3 = ((bf16[8,4,2048]{2,1,0:T(4,128)(2,1)}), bf16[8,4,2048]{2,1,0:T(4,128)(2,1)S(1)}, u32[]{:S(2)}, u32[]{:S(2)}) async-start(bf16[8,4,2048]{2,1,0:T(4,128)(2,1)} %broadcast_in_dim.89), calls=%async_computation.3 | async-start | bytes 262144 | tf_op jit(solution)/shard_map/all_to_all | solution.py:22
  201.4 13.3 %copy-start.7 = (f32[32,6]{0,1:T(8,128)S(1)}, f32[32,6]{0,1:T(8,128)}, u32[]{:S(2)}) copy-start(f32[32,6]{0,1:T(8,128)} %param.24) | copy-start | bytes 2308
  208.7 18.4 %all-to-all-start.5 = ((bf16[64,2,1024]{2,1,0:T(2,128)(2,1)}), bf16[64,2,1024]{2,1,0:T(2,128)(2,1)S(1)}, u32[]{:S(2)}, u32[]{:S(2)}) async-start(bf16[64,2,1024]{2,1,0:T(2,128)(2,1)} %reshape.189), calls=%async_computation.5 | async-start | bytes 524288 | tf_op jit(solution)/shard_map/all_to_all | solution.py:183
Sparse Core Ops, SparseCore 0:
  9.6 82.7 all-gather.1
where the time goes:
time: 247 us
  blocking collectives  78.3 us (32%)
  waiting for transfers between devices  68.9 us (28%)
  starting transfers between devices  54.4 us (22%)
  between operations  13.7 us (6%)
  matrix products  13.4 us (5%)
  other arithmetic  9.41 us (4%)
  local copies, waits for them, and re-layouts  8.5 us (3%)
    psum x2, blocking collectives, one_axis_at_a_time(): return functools.reduce(lax.psum, axes, shard)  44.7 us
    all_to_all x1, waiting for transfers between devices, sum_at_owner(): lax.all_to_all(blocks, axis, split_axis=0, concat_axis=0, tiled=True)  37.7 us
    all_to_all x2, starting transfers between devices, copy_for_each(): return lax.all_to_all(copies, axis, split_axis=0, concat_axis=0, tiled=True)  34.7 us
    all_to_all x1, blocking collectives, local(): lax.all_to_all(outgoing, EXPERT, split_axis=0, concat_axis=0, tiled=True)  22.4 us
    all_to_all x1, waiting for transfers between devices, local(): lax.all_to_all(result.reshape(experts, share_size, model_width).astype(jn...  11.8 us
    all_to_all x1, blocking collectives, summed_on_arrival(): lax.all_to_all(blocks, axis, split_axis=0, concat_axis=0, tiled=True)  11.2 us
    all_to_all x2, waiting for transfers between devices, copy_for_each(): return lax.all_to_all(copies, axis, split_axis=0, concat_axis=0, tiled=True)  10.5 us
    all_to_all x1, waiting for transfers between devices, local(): lax.all_to_all(latent_out, EXPERT, split_axis=1, concat_axis=0, tiled=True)  8.88 us
  transfers between devices with their start and end apart: 6, of which 5 were waited for; matrix products, arithmetic and copies ran while one was open for 6% of the time, Pallas kernels for 0%

commit v1 on v0

--- a/solution.py
+++ b/solution.py
@@ -112,32 +112,49 @@
     latent_out = jax.vmap(attend_one)(q_latent, latent_cache, lengths).reshape(
         requests, head_count * LAT
     )
-    pieces = lax.all_to_all(latent_out, EXPERT, split_axis=1, concat_axis=0, tiled=True)
-    group_ids = gathered_copies(adapter_ids, EXPERT, 0)
-    group_rows = pieces.shape[0]
     adapters = adapter_down.shape[1] // ADAPTER_RANK
     owned_count = adapter_up_factors.shape[0] // ADAPTER_RANK
-    down_projected_rows = jnp.dot(pieces, adapter_down, preferred_element_type=jnp.float32).reshape(
-        group_rows, adapters, ADAPTER_RANK
-    )
-    chosen_adapters = group_ids[:, None] == jnp.arange(adapters, dtype=jnp.int32)[None, :]
-    adapter_output = jnp.sum(
-        jnp.where(chosen_adapters[:, :, None], down_projected_rows, 0.0), axis=1
-    )
-    adapter_down_rows = one_axis_at_a_time(adapter_output, EXPERT)
-    adapter_scaled_output = (ADAPTER_SCALE * adapter_down_rows).astype(jnp.bfloat16)
-    first_owned = lax.axis_index(EXPERT) * owned_count
-    holder_mask = (
-        group_ids[:, None] == first_owned + jnp.arange(owned_count, dtype=jnp.int32)[None, :]
-    )
+    owners = lax.axis_size(EXPERT)
+    depth = adapter_down.shape[0]
+    sent = jnp.moveaxis(latent_out.reshape(requests, owners, depth), 1, 0)
+    sent_ids = jnp.broadcast_to(
+        adapter_ids.astype(jnp.bfloat16)[None, :, None], (owners, requests, depth)
+    )
+    arrived = lax.all_to_all(
+        jnp.concatenate([sent, sent_ids], axis=1), EXPERT, split_axis=0, concat_axis=0, tiled=True
+    )
+    pieces = arrived.reshape(owners * 2 * requests, depth)
+    group_ids = arrived[:, requests:, 0].astype(jnp.int32)
+    row_ids = jnp.concatenate([group_ids, jnp.full_like(group_ids, -1)], axis=1).reshape(-1)
+    down_rows = jnp.dot(pieces, adapter_down, preferred_element_type=jnp.float32).reshape(
+        -1, adapters, ADAPTER_RANK
+    )
+    chosen = row_ids[:, None] == jnp.arange(adapters, dtype=jnp.int32)[None, :]
+    lora_down = jnp.sum(jnp.where(chosen[:, :, None], down_rows, 0.0), axis=1)
+    lora_down = lora_down.reshape(owners, 2 * requests, ADAPTER_RANK)[:, :requests]
+    lora_down = lora_down.reshape(owners * requests, ADAPTER_RANK).T
+    for axis in EXPERT:
+        lora_down = copy_for_each(lora_down, axis).sum(axis=0)
+    lora_scaled = (ADAPTER_SCALE * lora_down.T).astype(jnp.bfloat16)
+    lora_scaled = jnp.pad(
+        lora_scaled.reshape(owners, requests, ADAPTER_RANK), ((0, 0), (0, requests), (0, 0))
+    ).reshape(-1, ADAPTER_RANK)
+    owned = lax.axis_index(EXPERT) * owned_count + jnp.arange(owned_count, dtype=jnp.int32)
     spread_rows = jnp.where(
-        holder_mask[:, :, None], adapter_scaled_output[:, None, :], jnp.zeros((), jnp.bfloat16)
-    ).reshape(group_rows, owned_count * ADAPTER_RANK)
-    attention = sum_at_owner(
-        jnp.dot(pieces, value_out, preferred_element_type=jnp.float32)
-        + jnp.dot(spread_rows, adapter_up_factors, preferred_element_type=jnp.float32),
-        EXPERT,
-        0,
+        (row_ids[:, None] == owned[None, :])[:, :, None],
+        lora_scaled[:, None, :],
+        jnp.zeros((), jnp.bfloat16),
+    ).reshape(-1, owned_count * ADAPTER_RANK)
+    partial = jnp.dot(pieces, value_out, preferred_element_type=jnp.float32) + jnp.dot(
+        spread_rows, adapter_up_factors, preferred_element_type=jnp.float32
+    )
+    partial = partial.reshape(owners, 2 * requests, model_width)[:, :requests]
+    attention = (
+        lax.all_to_all(
+            partial.astype(jnp.bfloat16), EXPERT, split_axis=0, concat_axis=0, tiled=True
+        )
+        .astype(jnp.float32)
+        .sum(axis=0)
     )
     residual_flow = residual.astype(jnp.float32) + attention
     inverse_rms = lax.rsqrt(

time: 247 us -> 189 us (0.77)
  blocking collectives: 78.3 us -> 29.6 us
  starting transfers between devices: 54.4 us -> 46.4 us
  waiting for transfers between devices: 68.9 us -> 62.6 us
  matrix products: 13.4 us -> 18.3 us
    psum x2 -> x0, blocking collectives: 44.7 us -> none  [one_axis_at_a_time(): return functools.reduce(lax.psum, axes, shard)]
    all_to_all x2 -> x3, starting transfers between devices: 34.7 us -> 18.6 us  [copy_for_each(): return lax.all_to_all(copies, axis, split_axis=0, concat_axis=0, tiled=True)]
    all_to_all x2, waiting for transfers between devices: 46.5 us -> 33 us  [the longest x1 21.8 us: local(): lax.all_to_all(partial.astype(jnp.bfloat16), EXPERT, split_axis=0, concat...]
    all_to_all x2, starting transfers between devices: 13.7 us -> 21.8 us  [the longest x1 17.1 us: local(): lax.all_to_all(jnp.concatenate([sent, sent_ids], axis=1), EXPERT, split_a...]
    all_to_all x2 -> x3, waiting for transfers between devices: 10.5 us -> 17.7 us  [copy_for_each(): return lax.all_to_all(copies, axis, split_axis=0, concat_axis=0, tiled=True)]
    all_to_all x1, blocking collectives: 22.4 us -> 18.4 us  [local(): lax.all_to_all(outgoing, EXPERT, split_axis=0, concat_axis=0, tiled=True)]
  transfers between devices with their start and end apart: 6 -> 7, of which waited for: 5 -> 6; matrix products, arithmetic and copies ran while one was open for 6% -> 11% of each run, Pallas kernels for 0% -> 0%
where the time goes in v1:
time: 189 us; the launch traced here: 188 us
  waiting for transfers between devices  62.6 us (33%)
  starting transfers between devices  46.4 us (25%)
  blocking collectives  29.6 us (16%)
  matrix products  18.3 us (10%)
  between operations  13.8 us (7%)
  other arithmetic  8.79 us (5%)
  local copies, waits for them, and re-layouts  8.75 us (5%)
    all_to_all x1, waiting for transfers between devices, local(): lax.all_to_all(partial.astype(jnp.bfloat16), EXPERT, split_axis=0, concat...  21.8 us
    all_to_all x3, starting transfers between devices, copy_for_each(): return lax.all_to_all(copies, axis, split_axis=0, concat_axis=0, tiled=True)  18.6 us
    all_to_all x1, blocking collectives, local(): lax.all_to_all(outgoing, EXPERT, split_axis=0, concat_axis=0, tiled=True)  18.4 us
    all_to_all x3, waiting for transfers between devices, copy_for_each(): return lax.all_to_all(copies, axis, split_axis=0, concat_axis=0, tiled=True)  17.7 us
    all_to_all x1, starting transfers between devices, local(): lax.all_to_all(jnp.concatenate([sent, sent_ids], axis=1), EXPERT, split_a...  17.1 us
    all_to_all x1, waiting for transfers between devices, local(): lax.all_to_all(result.reshape(experts, share_size, model_width).astype(jn...  11.8 us
    all_to_all x1, blocking collectives, summed_on_arrival(): lax.all_to_all(blocks, axis, split_axis=0, concat_axis=0, tiled=True)  11.2 us
    all_to_all x1, waiting for transfers between devices, local(): lax.all_to_all(jnp.concatenate([sent, sent_ids], axis=1), EXPERT, split_a...  11.2 us
  transfers between devices with their start and end apart: 7, of which 6 were waited for; matrix products, arithmetic and copies ran while one was open for 11% of the time, Pallas kernels for 0%

profile of v1, /device:TPU:1, one launch (start us, length us, event | category | flops | bytes accessed | tf_op | source)
XLA Modules:
  0.0 188.2 jit_solution(15602685742617303361)
XLA Ops:
  6.5 2.8 %pad_maximum_fusion = bf16[3,2048,128]{2,1,0:T(8,128)(2,1)} fusion(bf16[1,2048,128]{2,1,0:T(8,128)(2,1)} %param.27, bf16[1,2048,128]{2,1,0:T(8,128)(2,1)} %param.26, bf16[1,2048,128]{2,1,0:T(8,128)(2,1)} %param.25), kind=kLoop, calls=%fused_computation.18 | loop fusion | flops 1572864 | bytes 3145728 | tf_op jit(solution)/shard_map/concatenate | solution.py:53
  9.4 0.1 iota_compare_fusion.5
  9.5 1.4 fusion.13
  10.9 0.2 fusion.44
  11.1 1.3 fusion.15
  12.4 0.9 reshape_reshape.3
  13.4 0.1 pad.16.clone
  13.4 0.7 pad_maximum_fusion.1
  14.2 17.1 %all-to-all-start = ((bf16[64,8,128]{2,1,0:T(8,128)(2,1)}), bf16[64,8,128]{2,1,0:T(8,128)(2,1)S(1)}, u32[]{:S(2)}, u32[]{:S(2)}) async-start(bf16[64,8,128]{2,1,0:T(8,128)(2,1)} %pad_maximum_fusion.1), calls=%async_computation | async-start | bytes 262144 | tf_op jit(solution)/shard_map/all_to_all | solution.py:123
  31.3 0.3 copy.84
  31.6 11.2 %all-to-all-done = bf16[64,8,128]{2,1,0:T(8,128)(2,1)S(1)} async-done(((bf16[64,8,128]{2,1,0:T(8,128)(2,1)}), bf16[64,8,128]{2,1,0:T(8,128)(2,1)S(1)}, u32[]{:S(2)}, u32[]{:S(2)}) %all-to-all-start) | async-done | bytes 131104 | tf_op jit(solution)/shard_map/all_to_all | solution.py:123
  42.9 0.1 copy.82
  43.0 0.1 copy.83
  43.1 0.1 reshape.185
  43.2 0.7 select_reduce_fusion
  44.0 0.1 copy.86
  44.2 0.7 broadcast_in_dim.96
  44.9 3.4 %all-to-all-start.1 = ((f32[8,16,256]{2,1,0:T(8,128)}), f32[8,16,256]{2,1,0:T(8,128)S(1)}, u32[]{:S(2)}, u32[]{:S(2)}) async-start(f32[8,16,256]{2,1,0:T(8,128)} %broadcast_in_dim.96), calls=%async_computation.1 | async-start | bytes 262144 | tf_op jit(solution)/shard_map/all_to_all | solution.py:22
  48.3 7.9 %all-to-all-done.1 = f32[8,16,256]{2,1,0:T(8,128)S(1)} async-done(((f32[8,16,256]{2,1,0:T(8,128)}), f32[8,16,256]{2,1,0:T(8,128)S(1)}, u32[]{:S(2)}, u32[]{:S(2)}) %all-to-all-start.1) | async-done | bytes 131104 | tf_op jit(solution)/shard_map/all_to_all | solution.py:22
  56.2 0.7 broadcast_in_dim.97
  56.8 3.4 %all-to-all-start.2 = ((f32[8,16,256]{2,1,0:T(8,128)}), f32[8,16,256]{2,1,0:T(8,128)S(1)}, u32[]{:S(2)}, u32[]{:S(2)}) async-start(f32[8,16,256]{2,1,0:T(8,128)} %broadcast_in_dim.97), calls=%async_computation.2 | async-start | bytes 262144 | tf_op jit(solution)/shard_map/all_to_all | solution.py:22
  60.2 2.7 %fusion.31 = f32[512,2048]{1,0:T(8,128)} fusion(bf16[128,2048]{1,0:T(8,128)(2,1)S(1)} %copy-done, bf16[64,8,128]{2,1,0:T(8,128)(2,1)S(1)} %all-to-all-done), kind=kOutput, calls=%fused_computation.43 | convolution fusion | flops 268435456 | bytes 4849664 | tf_op jit(solution)/shard_map/dot_general | solution.py:148
  63.0 5.2 %all-to-all-done.2 = f32[8,16,256]{2,1,0:T(8,128)S(1)} async-done(((f32[8,16,256]{2,1,0:T(8,128)}), f32[8,16,256]{2,1,0:T(8,128)S(1)}, u32[]{:S(2)}, u32[]{:S(2)}) %all-to-all-start.2) | async-done | bytes 131104 | tf_op jit(solution)/shard_map/all_to_all | solution.py:22
  68.2 0.1 copy.88
  68.4 0.1 copy.89
  68.5 2.9 %fusion.4 = bf16[64,8,2048]{2,1,0:T(8,128)(2,1)S(1)} fusion(f32[512,2048]{1,0:T(8,128)} %fusion.31, bf16[512,32]{0,1:T(8,128)(2,1)S(1)} %bitcast.94, bf16[32,2048]{1,0:T(8,128)(2,1)S(1)} %copy-done.4), kind=kOutput, calls=%fused_computation.9 | convolution fusion | flops 69206016 | bytes 6455296 | tf_op jit(solution)/shard_map/dot_general | solution.py:148
  71.4 1.6 slice.43
  73.0 4.7 %all-to-all-start.3 = ((bf16[64,4,2048]{2,1,0:T(4,128)(2,1)}), bf16[64,4,2048]{2,1,0:T(4,128)(2,1)S(1)}, u32[]{:S(2)}, u32[]{:S(2)}) async-start(bf16[64,4,2048]{2,1,0:T(4,128)(2,1)} %slice.43), calls=%async_computation.3 | async-start | bytes 2097152 | tf_op jit(solution)/shard_map/all_to_all | solution.py:153
  77.7 0.1 copy.90
  77.8 0.1 eq.102
  77.9 0.6 reduce-window.6
  78.6 0.2 slice_reduce_fusion
  78.8 0.1 bitcast_bitcast_fusion
  78.9 0.1 eq.109
  79.0 0.1 iota_compare_fusion.2
  79.1 0.1 iota_compare_fusion.1
  79.2 21.8 %all-to-all-done.3 = bf16[64,4,2048]{2,1,0:T(4,128)(2,1)S(1)} async-done(((bf16[64,4,2048]{2,1,0:T(4,128)(2,1)}), bf16[64,4,2048]{2,1,0:T(4,128)(2,1)S(1)}, u32[]{:S(2)}, u32[]{:S(2)}) %all-to-all-start.3) | async-done | bytes 1048608 | tf_op jit(solution)/shard_map/all_to_all | solution.py:153
  101.1 0.4 convert_reduce_fusion
  101.5 0.1 multiply_reduce_fusion
  101.7 0.1 multiply_convert_fusion
  101.8 0.7 broadcast_in_dim.103
  102.4 11.8 %all-to-all-start.4 = ((bf16[8,4,2048]{2,1,0:T(4,128)(2,1)}), bf16[8,4,2048]{2,1,0:T(4,128)(2,1)S(1)}, u32[]{:S(2)}, u32[]{:S(2)}) async-start(bf16[8,4,2048]{2,1,0:T(4,128)(2,1)} %broadcast_in_dim.103), calls=%async_computation.4 | async-start | bytes 262144 | tf_op jit(solution)/shard_map/all_to_all | solution.py:22
  114.3 0.3 and_reduce_fusion
  114.6 0.2 copy.95
  114.8 0.1 copy.96
  114.9 4.6 %all-to-all-done.4 = bf16[8,4,2048]{2,1,0:T(4,128)(2,1)S(1)} async-done(((bf16[8,4,2048]{2,1,0:T(4,128)(2,1)}), bf16[8,4,2048]{2,1,0:T(4,128)(2,1)S(1)}, u32[]{:S(2)}, u32[]{:S(2)}) %all-to-all-start.4) | async-done | bytes 131104 | tf_op jit(solution)/shard_map/all_to_all | solution.py:22
  119.6 0.3 fusion.7
  119.8 0.5 broadcast.123
  120.3 0.8 reduce.2
  121.1 0.2 reshape.190
  121.3 18.4 %all_to_all.40 = bf16[64,2,1024]{2,1,0:T(2,128)(2,1)S(1)} all-to-all(bf16[64,2,1024]{2,1,0:T(2,128)(2,1)S(1)} %reshape.190), channel_id=1, replica_groups=mesh['dp'=8,'expert_0'=8,'expert_1'=8] {'expert_0','expert_1'}, dimensions={0} | all-to-all | bytes 524288 | tf_op jit(solution)/shard_map/all_to_all | solution.py:193
  139.7 0.2 reshape.191
  139.9 3.1 %fusion.3 = f32[64,1024]{1,0:T(8,128)S(1)} fusion(bf16[3,2048,1024]{2,1,0:T(8,128)(2,1)} %all-gather.2.cloned.1.call-done, bf16[64,1,2048]{2,1,0:T(2,128)(2,1)S(1)} %reshape.191), kind=kOutput, calls=%fused_computation.6 | convolution fusion | flops 268435456 | bytes 4718592 | tf_op jit(solution)/shard_map/dot_general | solution.py:85
  143.0 5.6 %fusion.6 = bf16[64,1,2048]{2,0,1:T(8,128)(2,1)S(1)} fusion(bf16[3,2048,1024]{2,1,0:T(8,128)(2,1)} %all-gather.2.cloned.1.call-done, f32[64,1024]{1,0:T(8,128)S(1)} %fusion.3, bf16[64,1,2048]{2,1,0:T(2,128)(2,1)S(1)} %reshape.191), kind=kOutput, calls=%fused_computation.12 | convolution fusion | flops 537395200 | bytes 9175040 | tf_op jit(solution)/shard_map/dot_general | solution.py:88
  148.6 0.8 reduce.3
  149.4 0.9 reshape.192
  150.3 6.0 %all-to-all-start.6 = ((bf16[64,2,1024]{2,1,0:T(2,128)(2,1)}), bf16[64,2,1024]{2,1,0:T(2,128)(2,1)S(1)}, u32[]{:S(2)}, u32[]{:S(2)}) async-start(bf16[64,2,1024]{2,1,0:T(2,128)(2,1)} %reshape.192), calls=%async_computation.6 | async-start | bytes 524288 | tf_op jit(solution)/shard_map/all_to_all | solution.py:200
  156.3 0.1 copy.94
  156.4 0.6 fusion.18
  157.0 11.8 %all-to-all-done.6 = bf16[64,2,1024]{2,1,0:T(2,128)(2,1)S(1)} async-done(((bf16[64,2,1024]{2,1,0:T(2,128)(2,1)}), bf16[64,2,1024]{2,1,0:T(2,128)(2,1)S(1)}, u32[]{:S(2)}, u32[]{:S(2)}) %all-to-all-start.6) | async-done | bytes 262176 | tf_op jit(solution)/shard_map/all_to_all | solution.py:200
  168.8 0.2 reshape.193
  169.0 0.4 convolution_convert_fusion.1
  169.4 11.2 %all_to_all.41 = bf16[8,4,2048]{2,1,0:T(4,128)(2,1)S(1)} all-to-all(bf16[8,4,2048]{2,1,0:T(4,128)(2,1)S(1)} %reshape.184), channel_id=1, replica_groups=mesh['dp'=8,'expert_0'=8,'expert_1'=8] {'dp'}, dimensions={0} | all-to-all | bytes 262144 | tf_op jit(solution)/shard_map/all_to_all | solution.py:63
  180.7 0.6 add_convert_fusion.1
  (49 shorter events, 0.8 us)
Async XLA Ops:
  6.5 53.7 %copy-start = (bf16[128,2048]{1,0:T(8,128)(2,1)S(1)}, bf16[128,2048]{1,0:T(8,128)(2,1)}, u32[]{:S(2)}) copy-start(bf16[128,2048]{1,0:T(8,128)(2,1)} %param.19) | copy-start | bytes 1572868
  6.5 2.9 %copy-start.8 = (s32[4]{0:T(128)S(1)}, s32[4]{0:T(128)}, u32[]{:S(2)}) copy-start(s32[4]{0:T(128)} %param.16) | copy-start | bytes 52
  6.5 3.0 %copy-start.1 = (bf16[4,512,576]{1,2,0:T(8,128)(2,1)S(1)}, bf16[4,512,576]{1,2,0:T(8,128)(2,1)}, u32[]{:S(2)}) copy-start(bf16[4,512,576]{1,2,0:T(8,128)(2,1)} %param.15) | copy-start | bytes 7077892
  6.5 133.4 %all-gather.2.cloned.1.call-start = ((), (), s32[]{:S(2)}) async-start(), calls=%async_computation.8 | async-start | bytes 14155776 | tf_op jit(solution)/shard_map/all_gather | solution.py:54
  9.4 4.0 %copy-start.9 = (s32[4]{0:T(128)S(1)}, s32[4]{0:T(128)}, u32[]{:S(2)}) copy-start(s32[4]{0:T(128)} %param.18) | copy-start | bytes 52
  9.4 21.9 %copy-start.2 = (bf16[128,2048]{1,0:T(8,128)(2,1)S(1)}, bf16[128,2048]{1,0:T(8,128)(2,1)}, u32[]{:S(2)}) copy-start(bf16[128,2048]{1,0:T(8,128)(2,1)} %param.20) | copy-start | bytes 1572868
  14.2 28.6 %all-to-all-start = ((bf16[64,8,128]{2,1,0:T(8,128)(2,1)}), bf16[64,8,128]{2,1,0:T(8,128)(2,1)S(1)}, u32[]{:S(2)}, u32[]{:S(2)}) async-start(bf16[64,8,128]{2,1,0:T(8,128)(2,1)} %pad_maximum_fusion.1), calls=%async_computation | async-start | bytes 262144 | tf_op jit(solution)/shard_map/all_to_all | solution.py:123
  44.0 24.5 %copy-start.4 = (bf16[32,2048]{1,0:T(8,128)(2,1)S(1)}, bf16[32,2048]{1,0:T(8,128)(2,1)}, u32[]{:S(2)}) copy-start(bf16[32,2048]{1,0:T(8,128)(2,1)} %param.21) | copy-start | bytes 393220
  44.9 11.3 %all-to-all-start.1 = ((f32[8,16,256]{2,1,0:T(8,128)}), f32[8,16,256]{2,1,0:T(8,128)S(1)}, u32[]{:S(2)}, u32[]{:S(2)}) async-start(f32[8,16,256]{2,1,0:T(8,128)} %broadcast_in_dim.96), calls=%async_computation.1 | async-start | bytes 262144 | tf_op jit(solution)/shard_map/all_to_all | solution.py:22
  56.8 11.3 %all-to-all-start.2 = ((f32[8,16,256]{2,1,0:T(8,128)}), f32[8,16,256]{2,1,0:T(8,128)S(1)}, u32[]{:S(2)}, u32[]{:S(2)}) async-start(f32[8,16,256]{2,1,0:T(8,128)} %broadcast_in_dim.97), calls=%async_computation.2 | async-start | bytes 262144 | tf_op jit(solution)/shard_map/all_to_all | solution.py:22
  68.5 9.2 %copy-start.5 = (bf16[2048]{0:T(1024)(128)(2,1)S(1)}, bf16[2048]{0:T(1024)(128)(2,1)}, u32[]{:S(2)}) copy-start(bf16[2048]{0:T(1024)(128)(2,1)} %param.22) | copy-start | bytes 12292
  68.5 9.2 %copy-start.6 = (s32[32,6]{0,1:T(8,128)S(1)}, s32[32,6]{0,1:T(8,128)}, u32[]{:S(2)}) copy-start(s32[32,6]{0,1:T(8,128)} %param.23) | copy-start | bytes 2308
  71.4 30.1 %copy-start.3 = (bf16[4,2048]{1,0:T(4,128)(2,1)S(1)}, bf16[4,2048]{1,0:T(4,128)(2,1)}, u32[]{:S(2)}) copy-start(bf16[4,2048]{1,0:T(4,128)(2,1)} %param.17) | copy-start | bytes 49156
  73.0 28.1 %all-to-all-start.3 = ((bf16[64,4,2048]{2,1,0:T(4,128)(2,1)}), bf16[64,4,2048]{2,1,0:T(4,128)(2,1)S(1)}, u32[]{:S(2)}, u32[]{:S(2)}) async-start(bf16[64,4,2048]{2,1,0:T(4,128)(2,1)} %slice.43), calls=%async_computation.3 | async-start | bytes 2097152 | tf_op jit(solution)/shard_map/all_to_all | solution.py:153
  102.4 17.1 %all-to-all-start.4 = ((bf16[8,4,2048]{2,1,0:T(4,128)(2,1)}), bf16[8,4,2048]{2,1,0:T(4,128)(2,1)S(1)}, u32[]{:S(2)}, u32[]{:S(2)}) async-start(bf16[8,4,2048]{2,1,0:T(4,128)(2,1)} %broadcast_in_dim.103), calls=%async_computation.4 | async-start | bytes 262144 | tf_op jit(solution)/shard_map/all_to_all | solution.py:22
  143.0 13.3 %copy-start.7 = (f32[32,6]{0,1:T(8,128)S(1)}, f32[32,6]{0,1:T(8,128)}, u32[]{:S(2)}) copy-start(f32[32,6]{0,1:T(8,128)} %param.24) | copy-start | bytes 2308
  150.3 18.5 %all-to-all-start.6 = ((bf16[64,2,1024]{2,1,0:T(2,128)(2,1)}), bf16[64,2,1024]{2,1,0:T(2,128)(2,1)S(1)}, u32[]{:S(2)}, u32[]{:S(2)}) async-start(bf16[64,2,1024]{2,1,0:T(2,128)(2,1)} %reshape.192), calls=%async_computation.6 | async-start | bytes 524288 | tf_op jit(solution)/shard_map/all_to_all | solution.py:200
Sparse Core Ops, SparseCore 0:
  9.5 82.7 all-gather.1

commit v2 on v0

v2 whole, which is shorter than its diff:
```python
import functools

import jax
import jax.numpy as jnp
from jax import lax
from jax.experimental import pallas as pl
from jax.experimental.pallas import tpu as pltpu
from jax.sharding import Mesh
from jax.sharding import PartitionSpec as P

LAT = 512
RANK = 16
EXPERT = ("expert_0", "expert_1")
EXPERT_DP = ("expert_0", "expert_1", "dp")
CUTS = 8
SOFTMAX_SCALE = 192.0 ** (-0.5)
ADAPTER_SCALE = 2.0
EPSILON = 1e-06
F32 = jnp.float32
BF16 = jnp.bfloat16
WHOLE = pl.BlockSpec(memory_space=pltpu.VMEM)
SCALARS = pl.BlockSpec(memory_space=pltpu.SMEM)
GRANT = pltpu.CompilerParams(vmem_limit_bytes=16 * 2**20)


def shape(dims, dtype):
    return jax.ShapeDtypeStruct(dims, dtype)


def call(kernel, outs, flops=10**7, nbytes=10**6):
    return functools.partial(
        pl.pallas_call,
        kernel,
        out_shape=outs,
        cost_estimate=pl.CostEstimate(flops=flops, bytes_accessed=nbytes, transcendentals=0),
        compiler_params=GRANT,
    )


def exchange(rows, axis):
    return lax.all_to_all(rows, axis, split_axis=0, concat_axis=0, tiled=True)


def index(dims, dim):
    return lax.broadcasted_iota(jnp.int32, dims, dim)


def one_hot(dims, hit):
    return jnp.where(hit(index(dims, 0), index(dims, 1)), 1.0, 0.0).astype(BF16)


def dot(a, b):
    return jnp.dot(a, b, preferred_element_type=F32)


def dot_t(a, b):
    return lax.dot_general(a, b, (((1,), (1,)), ((), ())), preferred_element_type=F32)


def attend_kernel(lengths, ids, query, cache, out, held):
    step, n = pl.program_id(0), pl.num_programs(0)
    heads = query.shape[1]
    scores = dot(query[0], cache[0]) * SOFTMAX_SCALE
    valid = index(scores.shape, 1) < lengths[step]
    scores = jnp.where(valid, scores, -1e30)
    raised = jnp.exp(scores - jnp.max(scores, axis=1, keepdims=True))
    weights = (raised / jnp.sum(raised, axis=1, keepdims=True)).astype(BF16)
    latents = dot_t(weights, cache[0, :LAT, :])
    lanes = out.shape[1]
    quarters = LAT // lanes
    for k in range(quarters):
        at = pl.multiple_of((step * quarters + k) * heads, heads)
        held[pl.ds(at, heads), :] = latents[:, k * lanes : (k + 1) * lanes].astype(BF16)

    @pl.when(step == n - 1)
    def _():
        rows, source = out.shape[0], held.shape[0]
        slots = 2 * 4

        def hit(o, c):
            owner, i = o // slots, o % slots
            want = i * (quarters * heads) + (owner % quarters) * heads + owner // quarters
            return (i < slots // 2) & (c == want)

        packed = dot(one_hot((rows, source), hit), held[...])
        i = index(packed.shape, 0) % slots
        for r in range(slots // 2):
            packed = jnp.where(i == slots // 2 + r, ids[r].astype(F32), packed)
        out[...] = packed.astype(BF16)


def attend(query, cache_t, lengths, ids, owners):
    n, heads, width = query.shape
    context = cache_t.shape[2]
    lanes = heads * LAT // owners
    return pl.pallas_call(
        attend_kernel,
        out_shape=shape((owners * 2 * n, lanes), BF16),
        grid_spec=pltpu.PrefetchScalarGridSpec(
            num_scalar_prefetch=2,
            grid=(n,),
            in_specs=[
                pl.BlockSpec((1, heads, width), lambda i, *_: (i, 0, 0)),
                pl.BlockSpec((1, width, context), lambda i, *_: (i, 0, 0)),
            ],
            out_specs=pl.BlockSpec((owners * 2 * n, lanes), lambda i, *_: (0, 0)),
            scratch_shapes=[pltpu.VMEM((n * heads * LAT // lanes, lanes), BF16)],
        ),
        cost_estimate=pl.CostEstimate(
            flops=4 * n * heads * width * context,
            bytes_accessed=2 * n * width * context,
            transcendentals=0,
        ),
        compiler_params=pltpu.CompilerParams(vmem_limit_bytes=53 * 2**20),
    )(lengths, ids, query, cache_t)


def lora_kernel(arrived, down, copies, pieces, numbers):
    rows = pieces.shape[0]
    lanes = arrived.shape[1]
    half = 4
    both = arrived[...]
    dims = (rows, 2 * rows)
    kept = dot(one_hot(dims, lambda o, c: c == (o // half) * 2 * half + o % half), both)
    named = dot(one_hot(dims, lambda o, c: c == (o // half) * 2 * half + half + o % half), both)
    kept = kept.astype(BF16)
    pieces[...] = kept
    numbers[...] = named.T[:8]
    total = jnp.zeros((rows, lanes), F32)
    group = index((rows, lanes), 1) // RANK
    own = named.astype(jnp.int32)
    for t in range(down.shape[1] // lanes):
        product = dot(kept, down[:, t * lanes : (t + 1) * lanes])
        total = total + jnp.where(own == group + t * (lanes // RANK), product, 0.0)
    shift = RANK
    while shift < lanes:
        total = total + pltpu.roll(total, shift, 1)
        shift *= 2
    turned = total.T[:RANK]
    for k in range(copies.shape[0]):
        copies[k] = turned


def resend_kernel(arrived, copies):
    total = jnp.sum(arrived[...], axis=0)
    for k in range(copies.shape[0]):
        copies[k] = total


def project_kernel(first, arrived, pieces, numbers, value, up, out):
    scaled = (ADAPTER_SCALE * jnp.sum(arrived[...], axis=0)).astype(BF16).astype(F32)
    number = numbers[:1].astype(jnp.int32)
    owned = up.shape[0] // RANK
    spread = [jnp.where(number == first[0] + k, scaled, 0.0) for k in range(owned)]
    spread = jnp.concatenate(spread, axis=0).T.astype(BF16)
    kept = pieces[...]
    homes, _, columns = out.shape
    rows = kept.shape[0]
    low = index((rows // 8, 8, columns), 1) < 4
    for pair in range(0, CUTS, 4):
        blocks = []
        for cut in range(pair, pair + 4):
            at = slice(cut * columns, (cut + 1) * columns)
            block = dot(kept, value[:, at]) + dot(spread, up[:, at])
            blocks.append(block.reshape(rows // 8, 8, columns))
        joined = []
        for a, b in (blocks[:2], blocks[2:]):
            even = jnp.where(low, a, pltpu.roll(b, 4, 1))
            odd = jnp.where(low, pltpu.roll(a, 4, 1), b)
            joined.append(jnp.stack([even, odd], axis=1).reshape(homes, 8, columns))
        both = jnp.concatenate(joined, axis=1)
        out[:, pair * 4 : (pair + 4) * 4, :] = both.astype(BF16)


def norm_kernel(arrived, residual, gain, stream, copies):
    flow = residual[...] + jnp.sum(arrived[...].astype(F32), axis=0)
    stream[...] = flow
    rows, columns = flow.shape
    squares = jnp.sum(flow * flow, axis=1, keepdims=True)
    for shift in (4, 8, 16):
        squares = squares + pltpu.roll(jnp.broadcast_to(squares, (rows, 128)), shift, 0)[:, :1]
    scale = lax.rsqrt(squares / (columns * CUTS) + EPSILON)
    normed = (flow * scale * gain[...]).astype(BF16)
    for k in range(copies.shape[0]):
        copies[k] = normed


def routes_kernel(routing, weights, pick, give):
    experts, tokens = routing.shape
    wide, long = tokens * CUTS, experts * CUTS
    to_expert = one_hot((long, experts), lambda o, c: o // CUTS == c)
    to_token = one_hot(
        (tokens, wide), lambda c, o: (o // (4 * CUTS) == c // 4) & (o % 4 == c % 4)
    )
    same = index((long, wide), 0) % CUTS == (index((long, wide), 1) // 4) % CUTS
    spread = dot(dot(to_expert, routing[...]).astype(BF16), to_token)
    pick[...] = jnp.where(same, spread, 0.0).astype(BF16)
    left = weights[...]
    for k in range(3):
        term = left.astype(BF16)
        left = left - term.astype(F32)
        spread = dot(dot(to_expert, term).astype(BF16), to_token)
        give[k] = jnp.where(same, spread, 0.0).astype(BF16)


def pick_kernel(pick, tokens, out):
    out[...] = dot(pick[...], tokens[...]).astype(BF16)


def give_kernel(give, rows, out):
    total = None
    for k in range(3):
        term = lax.dot_general(
            give[k], rows[...], (((0,), (0,)), ((), ())), preferred_element_type=F32
        )
        total = term if total is None else total + term
    out[...] = total.astype(BF16)


def ffn_kernel(rows, gate, up, down, out, gate_here, up_here, down_here, done):
    length, columns = rows.shape
    slots = length // CUTS
    parts = [slice(at, at + columns) for at in range(0, gate.shape[1], columns)]
    pairs = ((gate, gate_here), (up, up_here), (down, down_here))
    fetches = [
        [
            pltpu.make_async_copy(source.at[:, part], target.at[:, part], done.at[k, n])
            for k, (source, target) in enumerate(pairs)
        ]
        for n, part in enumerate(parts)
    ]
    for fetch in fetches:
        for copy in fetch:
            copy.start()
    apart = one_hot((length, length), lambda o, c: c == (o % slots) * CUTS + o // slots)
    apart = dot(apart, rows[...]).astype(BF16)
    tokens = jnp.concatenate(
        [apart[cut * slots : (cut + 1) * slots] for cut in range(CUTS)], axis=1
    )
    total = None
    for part, fetch in zip(parts, fetches):
        fetch[0].wait()
        gated = dot(tokens, gate_here[:, part])
        fetch[1].wait()
        raised = dot(tokens, up_here[:, part])
        acted = (gated / (1.0 + jnp.exp(-gated)) * raised).astype(BF16)
        fetch[2].wait()
        term = dot_t(acted, down_here[:, part])
        total = term if total is None else total + term
    result = total.astype(BF16)
    stacked = jnp.concatenate(
        [result[:, cut * columns : (cut + 1) * columns] for cut in range(CUTS)], axis=0
    )
    joint = one_hot((length, length), lambda o, c: c == (o % CUTS) * slots + o // CUTS)
    out[...] = dot(joint, stacked).astype(BF16)


def ffn(rows, gate, up, down):
    width, hidden = gate.shape
    slots, columns = rows.shape[0] // CUTS, rows.shape[1]
    return pl.pallas_call(
        ffn_kernel,
        out_shape=shape(rows.shape, BF16),
        in_specs=[WHOLE] + [pl.BlockSpec(memory_space=pl.ANY)] * 3,
        out_specs=WHOLE,
        scratch_shapes=[pltpu.VMEM((width, hidden), BF16)] * 3
        + [pltpu.SemaphoreType.DMA((3, hidden // columns))],
        cost_estimate=pl.CostEstimate(
            flops=6 * slots * width * hidden,
            bytes_accessed=6 * width * hidden,
            transcendentals=0,
        ),
        compiler_params=pltpu.CompilerParams(vmem_limit_bytes=50 * 2**20),
    )(rows, gate, up, down)


def final_kernel(arrived, stream, out):
    total = stream[...] + jnp.sum(arrived[...].astype(F32), axis=0)
    columns = total.shape[1]
    n = out.shape[0]
    for cut in range(CUTS):
        out[:, cut * columns : (cut + 1) * columns] = total[cut * n : (cut + 1) * n].astype(BF16)


def local(
    q_latent,
    latent_cache,
    lengths,
    residual,
    adapter_ids,
    value_out,
    adapter_down,
    adapter_up_factors,
    norm_gain,
    expert_ids,
    gate_weights,
    w_gate,
    w_up,
    w_down,
):
    requests, model_width = residual.shape
    owners = lax.axis_size(EXPERT)
    dp_count = lax.axis_size("dp")
    columns = model_width // CUTS
    group = owners * requests
    owned_count = adapter_up_factors.shape[0] // RANK
    packed = attend(q_latent, jnp.swapaxes(latent_cache, 1, 2), lengths, adapter_ids, owners)
    lanes = packed.shape[1]
    first = (lax.axis_index(EXPERT) * owned_count).astype(jnp.int32).reshape(1)
    packed, first = lax.optimization_barrier((packed, first))
    arrived = exchange(packed.reshape(owners, 2 * requests, lanes), EXPERT)
    arrived = arrived.reshape(owners * 2 * requests, lanes)
    side = lax.axis_size(EXPERT[0])
    copies, pieces, numbers = call(
        lora_kernel,
        (
            shape((side, RANK, group), F32),
            shape((group, lanes), BF16),
            shape((8, group), F32),
        ),
    )(in_specs=[WHOLE, WHOLE], out_specs=(WHOLE, WHOLE, WHOLE))(arrived, adapter_down)
    half = exchange(copies, EXPERT[0])
    copies = call(resend_kernel, shape((side, RANK, group), F32))(
        in_specs=[WHOLE], out_specs=WHOLE
    )(half)
    summed = exchange(copies, EXPERT[1])
    partial = call(project_kernel, shape((owners, CUTS * requests, columns), BF16))(
        in_specs=[SCALARS, WHOLE, WHOLE, WHOLE, WHOLE, WHOLE], out_specs=WHOLE
    )(first, summed, pieces, numbers, value_out, adapter_up_factors)
    at_home = exchange(partial, EXPERT)

    tokens, top_count = expert_ids.shape
    experts = owners * w_gate.shape[0]
    position = lax.axis_index("dp")
    member = expert_ids[:, :, None] == jnp.arange(experts, dtype=jnp.int32)[None, None, :]
    flat_hits = member.reshape(tokens * top_count, experts).astype(jnp.int32)
    slot_rank = jnp.sum((jnp.cumsum(flat_hits, axis=0) - 1) * flat_hits, axis=1).reshape(
        tokens, top_count
    )
    mine = member & (slot_rank == position)[:, :, None]
    routing = jnp.any(mine, axis=1).astype(BF16).T
    weights = jnp.sum(jnp.where(mine, gate_weights[:, :, None], 0.0), axis=1).T
    wide, long = tokens * CUTS, experts * CUTS
    pick, give = call(
        routes_kernel, (shape((long, wide), BF16), shape((3, long, wide), BF16))
    )(in_specs=[WHOLE, WHOLE], out_specs=(WHOLE, WHOLE))(routing, weights)

    def cut_rows(rows):
        return jnp.moveaxis(rows.reshape(-1, CUTS, columns), 1, 0)

    residual_cut = cut_rows(residual.astype(F32)).reshape(CUTS * requests, columns)
    gain_cut = jnp.broadcast_to(
        cut_rows(norm_gain.astype(F32)), (CUTS, requests, columns)
    ).reshape(CUTS * requests, columns)
    at_home, pick, give, residual_cut, gain_cut = lax.optimization_barrier(
        (at_home, pick, give, residual_cut, gain_cut)
    )
    stream, copies = call(
        norm_kernel,
        (shape((CUTS * requests, columns), F32), shape((dp_count, CUTS * requests, columns), BF16)),
    )(in_specs=[WHOLE, WHOLE, WHOLE], out_specs=(WHOLE, WHOLE))(at_home, residual_cut, gain_cut)
    column = exchange(copies, "dp").reshape(wide, columns)
    outgoing = call(pick_kernel, shape((long, columns), BF16))(
        in_specs=[WHOLE, WHOLE], out_specs=WHOLE
    )(pick, column)
    gathered = [lax.all_gather(w[0], "dp", axis=1, tiled=True) for w in (w_gate, w_up, w_down)]
    own_share = exchange(outgoing.reshape(experts, CUTS, columns), EXPERT).reshape(long, columns)
    result = ffn(own_share, *gathered)
    returned = exchange(result.reshape(experts, CUTS, columns), EXPERT).reshape(long, columns)
    routed = call(give_kernel, shape((wide, columns), BF16))(
        in_specs=[WHOLE, WHOLE], out_specs=WHOLE
    )(give, returned)
    terms = exchange(routed.reshape(dp_count, CUTS * requests, columns), "dp")
    return call(final_kernel, shape((requests, model_width), BF16))(
        in_specs=[WHOLE, WHOLE], out_specs=WHOLE
    )(terms, stream)


def solution(mesh):
    split = Mesh(mesh.devices.reshape(mesh.shape["dp"], 8, 8), ("dp", "expert_0", "expert_1"))
    in_specs = (
        P(EXPERT_DP, None, None),
        P(EXPERT_DP, None, None),
        P(EXPERT_DP),
        P(EXPERT_DP, None),
        P(EXPERT_DP),
        P(EXPERT, None),
        P(EXPERT, None),
        P(EXPERT, None),
        P(),
        P(EXPERT, None),
        P(EXPERT, None),
        P(EXPERT, None, "dp"),
        P(EXPERT, None, "dp"),
        P(EXPERT, None, "dp"),
    )
    out_specs = P(EXPERT_DP, None)
    return jax.shard_map(local, mesh=split, in_specs=in_specs, out_specs=out_specs, check_vma=False)
```

time: 247 us -> 197 us (0.80)
  starting transfers between devices: 54.4 us -> 4.73 us
  blocking collectives: 78.3 us -> 122 us
  waiting for transfers between devices: 68.9 us -> 35.2 us
  Pallas kernels: 0 us -> 17.1 us
  matrix products: 13.4 us -> 0 us
  other arithmetic: 9.41 us -> 1.1 us
  local copies, waits for them, and re-layouts: 8.5 us -> 3.02 us
    all_to_all x2 -> x7, blocking collectives: 33.6 us -> 122 us  [exchange(): return lax.all_to_all(rows, axis, split_axis=0, concat_axis=0, tiled=True)]
    all_to_all x5 -> x1, starting transfers between devices: 54.4 us -> 4.65 us  [exchange(): return lax.all_to_all(rows, axis, split_axis=0, concat_axis=0, tiled=True)]
    all_to_all x5 -> x1, waiting for transfers between devices: 68.8 us -> 20.3 us  [exchange(): return lax.all_to_all(rows, axis, split_axis=0, concat_axis=0, tiled=True)]
    psum x2 -> x0, blocking collectives: 44.7 us -> none  [one_axis_at_a_time(): return functools.reduce(lax.psum, axes, shard)]
    pallas_call x0 -> x10, Pallas kernels: none -> 17.1 us  [the longest x1 7.06 us: ffn(): pl.pallas_call(ffn_kernel, out_shape=shape(rows.shape, BF16), in_specs=[W...]
    dot_general x9 -> x0, matrix products: 13.4 us -> none  [the longest x1 5.63 us: expert_rows(): lax.dot_general(hidden_bf, down_part, (((1,), (1,)), ((), ())), preferred...]
    all_gather x1 -> x3, waiting for transfers between devices: 0.02 us -> 12.8 us  [local(): lax.all_gather(w[0], 'dp', axis=1, tiled=True)]
    concatenate x1 -> x0, other arithmetic: 2.86 us -> none  [in_one_piece(): both = jnp.concatenate(arrays, axis=along)]
  transfers between devices with their start and end apart: 6 -> 4, of which waited for: 5 -> 2; matrix products, arithmetic and copies ran while one was open for 6% -> 1% of each run, Pallas kernels for 0% -> 5%
where the time goes in v2:
time: 197 us; the launch traced here: 196 us
  blocking collectives  122 us (62%)
  waiting for transfers between devices  35.2 us (18%)
  Pallas kernels  17.1 us (9%)
  between operations  13.3 us (7%)
  starting transfers between devices  4.73 us (2%)
  local copies, waits for them, and re-layouts  3.02 us (2%)
    all_to_all x7, blocking collectives, exchange(): return lax.all_to_all(rows, axis, split_axis=0, concat_axis=0, tiled=True)  122 us
    all_to_all x1, waiting for transfers between devices, exchange(): return lax.all_to_all(rows, axis, split_axis=0, concat_axis=0, tiled=True)  20.3 us
    all_gather x3, waiting for transfers between devices, local(): lax.all_gather(w[0], 'dp', axis=1, tiled=True)  12.8 us
    pallas_call x1, Pallas kernels, ffn(): pl.pallas_call(ffn_kernel, out_shape=shape(rows.shape, BF16), in_specs=[W...  7.06 us
    pallas_call x1, Pallas kernels, attend(): pl.pallas_call(attend_kernel, out_shape=shape((owners * 2 * n, lanes), BF...  4.68 us
    all_to_all x1, starting transfers between devices, exchange(): return lax.all_to_all(rows, axis, split_axis=0, concat_axis=0, tiled=True)  4.65 us
  transfers between devices with their start and end apart: 4, of which 2 were waited for; matrix products, arithmetic and copies ran while one was open for 1% of the time, Pallas kernels for 5%

profile of v2, /device:TPU:1, one launch (start us, length us, event | category | flops | bytes accessed | tf_op | source)
XLA Modules:
  0.0 196.4 jit_solution(7905204219558509302)
XLA Ops:
  6.5 0.0 copy-start
  6.5 0.0 copy-start.1
  6.5 0.0 copy-start.2
  6.5 0.0 all-gather.7.cloned.1.call-start
  6.5 0.7 all-gather.7.cloned.1.call-update
  7.3 0.0 all-gather.9.cloned.1.call-start
  7.3 0.7 all-gather.9.cloned.1.call-update
  8.0 0.0 all-gather.11.cloned.1.call-start
  8.1 0.7 all-gather.11.cloned.1.call-update
  8.7 0.0 copy-start.6
  8.8 0.0 copy-start.3
  8.8 0.9 copy-done.3
  9.7 0.0 copy-start.4
  9.7 0.7 copy-done.4
  10.3 0.0 copy-start.5
  10.3 0.7 copy-done.5
  11.0 0.0 copy-start.8
  11.0 0.0 copy-start.7
  11.0 0.0 copy-start.9
  11.0 4.7 %shard_map.136 = bf16[512,128]{1,0:T(8,128)(2,1)S(1)} custom-call(s32[4]{0:T(128)S(1)} %copy-done.4, s32[4]{0:T(128)S(1)} %copy-done.5, bf16[4,16,576]{2,1,0:T(8,128)(2,1)S(1)} %copy-done.3, bf16[4,576,512]{2,1,0:T(8,128)(2,1)} %bitcast.44), custom_call_target="tpu_custom_call" | custom-call | flops 75497472 | bytes 2359296 | tf_op jit(solution)/shard_map/pallas_call | solution.py:96
  15.7 28.4 %all_to_all.40 = bf16[64,8,128]{2,1,0:T(8,128)(2,1)S(1)} all-to-all(bf16[64,8,128]{2,1,0:T(8,128)(2,1)S(1)} %bitcast.38), channel_id=1, replica_groups=mesh['dp'=8,'expert_0'=8,'expert_1'=8] {'expert_0','expert_1'}, dimensions={0} | all-to-all | bytes 262144 | tf_op jit(solution)/shard_map/all_to_all | solution.py:41
  44.1 0.0 copy-done
  44.1 0.9 shard_map.137
  45.0 10.4 %all_to_all.41.arrived = f32[8,16,256]{2,1,0:T(8,128)S(1)} all-to-all(f32[8,16,256]{2,1,0:T(8,128)S(1)} %get-tuple-element.21), channel_id=1, replica_groups=mesh['dp'=8,'expert_0'=8,'expert_1'=8] {'expert_0'}, dimensions={0} | all-to-all | bytes 262144 | tf_op jit(solution)/shard_map/all_to_all | solution.py:41
  55.4 10.4 %all_to_all.42.arrived = f32[8,16,256]{2,1,0:T(8,128)S(1)} all-to-all(f32[8,16,256]{2,1,0:T(8,128)S(1)} %shard_map.138), channel_id=1, replica_groups=mesh['dp'=8,'expert_0'=8,'expert_1'=8] {'expert_1'}, dimensions={0} | all-to-all | bytes 262144 | tf_op jit(solution)/shard_map/all_to_all | solution.py:41
  65.9 0.0 copy-done.1
  65.9 0.0 copy-done.2
  65.9 1.8 shard_map.139
  67.7 4.7 %all-to-all-start.3 = ((bf16[64,32,256]{2,1,0:T(8,128)(2,1)}), bf16[64,32,256]{2,1,0:T(8,128)(2,1)S(1)}, u32[]{:S(2)}, u32[]{:S(2)}) async-start(bf16[64,32,256]{2,1,0:T(8,128)(2,1)} %shard_map.139), calls=%async_computation.3 | async-start | bytes 2097152 | tf_op jit(solution)/shard_map/all_to_all | solution.py:41
  72.3 0.0 copy-done.6
  72.3 0.1 copy.31
  72.4 0.1 eq.45
  72.6 0.6 reduce-window.6
  73.2 0.2 slice_reduce_fusion
  73.4 0.1 bitcast_bitcast_fusion
  73.5 0.1 eq.54
  73.7 0.1 copy.34
  73.8 0.1 fusion.1
  73.9 0.1 copy.35
  74.0 0.0 copy-done.8
  74.0 0.1 select_reduce_fusion
  74.2 0.1 copy.36
  74.2 0.0 copy-done.7
  74.3 0.0 copy-done.9
  74.3 0.8 shard_map.140
  75.2 20.3 %all-to-all-done.3.arrived = bf16[64,32,256]{2,1,0:T(8,128)(2,1)S(1)} async-done(((bf16[64,32,256]{2,1,0:T(8,128)(2,1)}), bf16[64,32,256]{2,1,0:T(8,128)(2,1)S(1)}, u32[]{:S(2)}, u32[]{:S(2)}) %all-to-all-start.3) | async-done | bytes 1048608 | tf_op jit(solution)/shard_map/all_to_all | solution.py:41
  95.5 0.5 shard_map.141
  96.0 16.8 %all_to_all.43 = bf16[8,32,256]{2,1,0:T(8,128)(2,1)S(1)} all-to-all(bf16[8,32,256]{2,1,0:T(8,128)(2,1)S(1)} %get-tuple-element.31), channel_id=1, replica_groups=mesh['dp'=8,'expert_0'=8,'expert_1'=8] {'dp'}, dimensions={0} | all-to-all | bytes 262144 | tf_op jit(solution)/shard_map/all_to_all | solution.py:41
  112.8 0.2 shard_map.142
  113.0 18.4 %all_to_all.44 = bf16[64,8,256]{2,1,0:T(8,128)(2,1)S(1)} all-to-all(bf16[64,8,256]{2,1,0:T(8,128)(2,1)S(1)} %bitcast.33), channel_id=1, replica_groups=mesh['dp'=8,'expert_0'=8,'expert_1'=8] {'expert_0','expert_1'}, dimensions={0} | all-to-all | bytes 524288 | tf_op jit(solution)/shard_map/all_to_all | solution.py:41
  131.4 0.0 all-gather.7.cloned.1.call-done
  131.4 0.0 all-gather.9.cloned.1.call-done
  131.4 12.8 %all-gather.11.cloned.1.call-done = bf16[1,2048,1024]{2,1,0:T(8,128)(2,1)} async-done(((bf16[1,2048,128]{2,1,0:T(8,128)(2,1)}), bf16[1,2048,1024]{2,1,0:T(8,128)(2,1)}) %all-gather.11.cloned.1.call-update) | async-done | bytes 4194320 | tf_op jit(solution)/shard_map/all_gather | solution.py:366
  144.2 7.1 %shard_map.143 = bf16[512,256]{1,0:T(8,128)(2,1)S(1)} custom-call(bf16[512,256]{1,0:T(8,128)(2,1)S(1)} %bitcast.31, bf16[2048,1024]{1,0:T(8,128)(2,1)} %bitcast.41, bf16[2048,1024]{1,0:T(8,128)(2,1)} %bitcast.42, bf16[2048,1024]{1,0:T(8,128)(2,1)} %bitcast.43), custom_call_target="tpu_custom_call" | custom-call | flops 805306368 | bytes 12582912 | tf_op jit(solution)/shard_map/pallas_call | solution.py:261
  151.2 26.0 %all_to_all.45 = bf16[64,8,256]{2,1,0:T(8,128)(2,1)S(1)} all-to-all(bf16[64,8,256]{2,1,0:T(8,128)(2,1)S(1)} %bitcast.32), channel_id=1, replica_groups=mesh['dp'=8,'expert_0'=8,'expert_1'=8] {'expert_0','expert_1'}, dimensions={0} | all-to-all | bytes 524288 | tf_op jit(solution)/shard_map/all_to_all | solution.py:41
  177.3 0.4 shard_map.144
  177.7 11.6 %all_to_all.46.arrived = bf16[8,32,256]{2,1,0:T(8,128)(2,1)S(1)} all-to-all(bf16[8,32,256]{2,1,0:T(8,128)(2,1)S(1)} %bitcast.37), channel_id=1, replica_groups=mesh['dp'=8,'expert_0'=8,'expert_1'=8] {'dp'}, dimensions={0} | all-to-all | bytes 262144 | tf_op jit(solution)/shard_map/all_to_all | solution.py:41
  189.3 0.6 shard_map.145
  (13 shorter events, 0.2 us)
Async XLA Ops:
  6.5 37.6 %copy-start = (bf16[128,2048]{1,0:T(8,128)(2,1)S(1)}, bf16[128,2048]{1,0:T(8,128)(2,1)}, u32[]{:S(2)}) copy-start(bf16[128,2048]{1,0:T(8,128)(2,1)} %down.1) | copy-start | bytes 1572868
  6.5 59.3 %copy-start.1 = (bf16[128,2048]{1,0:T(8,128)(2,1)S(1)}, bf16[128,2048]{1,0:T(8,128)(2,1)}, u32[]{:S(2)}) copy-start(bf16[128,2048]{1,0:T(8,128)(2,1)} %value.1) | copy-start | bytes 1572868
  6.5 59.3 %copy-start.2 = (bf16[32,2048]{1,0:T(8,128)(2,1)S(1)}, bf16[32,2048]{1,0:T(8,128)(2,1)}, u32[]{:S(2)}) copy-start(bf16[32,2048]{1,0:T(8,128)(2,1)} %up.1) | copy-start | bytes 393220
  6.5 124.8 %all-gather.7.cloned.1.call-start = ((), (), s32[]{:S(2)}) async-start(), calls=%async_computation.8 | async-start | bytes 4718592 | tf_op jit(solution)/shard_map/all_gather | solution.py:366
  7.3 124.1 %all-gather.9.cloned.1.call-start = ((), (), s32[]{:S(2)}) async-start(), calls=%async_computation.9 | async-start | bytes 4718592 | tf_op jit(solution)/shard_map/all_gather | solution.py:366
  8.0 136.2 %all-gather.11.cloned.1.call-start = ((), (), s32[]{:S(2)}) async-start(), calls=%async_computation.10 | async-start | bytes 4718592 | tf_op jit(solution)/shard_map/all_gather | solution.py:366
  8.7 63.6 %copy-start.6 = (s32[32,6]{0,1:T(8,128)S(1)}, s32[32,6]{0,1:T(8,128)}, u32[]{:S(2)}) copy-start(s32[32,6]{0,1:T(8,128)} %param.23) | copy-start | bytes 2308
  8.8 0.9 copy-start.3
  9.7 0.7 copy-start.4
  10.3 0.7 copy-start.5
  11.0 63.0 %copy-start.8 = (f32[32,6]{0,1:T(8,128)S(1)}, f32[32,6]{0,1:T(8,128)}, u32[]{:S(2)}) copy-start(f32[32,6]{0,1:T(8,128)} %param.24) | copy-start | bytes 2308
  11.0 63.3 %copy-start.7 = (bf16[4,2048]{1,0:T(4,128)(2,1)S(1)}, bf16[4,2048]{1,0:T(4,128)(2,1)}, u32[]{:S(2)}) copy-start(bf16[4,2048]{1,0:T(4,128)(2,1)} %param.17) | copy-start | bytes 49156
  11.0 63.3 %copy-start.9 = (bf16[2048]{0:T(1024)(128)(2,1)S(1)}, bf16[2048]{0:T(1024)(128)(2,1)}, u32[]{:S(2)}) copy-start(bf16[2048]{0:T(1024)(128)(2,1)} %param.22) | copy-start | bytes 12292
  67.7 27.9 %all-to-all-start.3 = ((bf16[64,32,256]{2,1,0:T(8,128)(2,1)}), bf16[64,32,256]{2,1,0:T(8,128)(2,1)S(1)}, u32[]{:S(2)}, u32[]{:S(2)}) async-start(bf16[64,32,256]{2,1,0:T(8,128)(2,1)} %shard_map.139), calls=%async_computation.3 | async-start | bytes 2097152 | tf_op jit(solution)/shard_map/all_to_all | solution.py:41
Sparse Core Ops, SparseCore 0:
  9.5 46.7 all-gather.6
  58.3 41.8 all-gather.8
  102.3 41.8 all-gather.10

commit v3 on v2

--- a/solution.py
+++ b/solution.py
@@ -18,6 +18,7 @@
 EPSILON = 1e-06
 F32 = jnp.float32
 BF16 = jnp.bfloat16
+FAR = pl.BlockSpec(memory_space=pltpu.HBM)
 WHOLE = pl.BlockSpec(memory_space=pltpu.VMEM)
 SCALARS = pl.BlockSpec(memory_space=pltpu.SMEM)
 GRANT = pltpu.CompilerParams(vmem_limit_bytes=16 * 2**20)
@@ -57,62 +58,88 @@
     return lax.dot_general(a, b, (((1,), (1,)), ((), ())), preferred_element_type=F32)
 
 
-def attend_kernel(lengths, ids, query, cache, out, held):
-    step, n = pl.program_id(0), pl.num_programs(0)
-    heads = query.shape[1]
-    scores = dot(query[0], cache[0]) * SOFTMAX_SCALE
-    valid = index(scores.shape, 1) < lengths[step]
-    scores = jnp.where(valid, scores, -1e30)
-    raised = jnp.exp(scores - jnp.max(scores, axis=1, keepdims=True))
-    weights = (raised / jnp.sum(raised, axis=1, keepdims=True)).astype(BF16)
-    latents = dot_t(weights, cache[0, :LAT, :])
+def attend_kernel(
+    lengths, ids, query, cache, *rest
+):
+    weights, (out, joined) = rest[:3], rest[3:5]
+    lengths_here, ids_here, query_here, cache_here, weights_here, small, big, side = rest[5:]
+    n, heads = query.shape[0], query.shape[1]
+    firsts = [
+        pltpu.make_async_copy(source, target, small.at[k])
+        for k, (source, target) in enumerate(
+            ((lengths, lengths_here), (ids, ids_here), (query, query_here))
+        )
+    ]
+    rows = [pltpu.make_async_copy(cache.at[r], cache_here.at[r], big.at[r]) for r in range(n)]
+    taken = [
+        pltpu.make_async_copy(w, weights_here.at[k], side.at[k]) for k, w in enumerate(weights)
+    ]
+    given = [
+        pltpu.make_async_copy(weights_here.at[k], joined.at[k], side.at[3 + k]) for k in range(3)
+    ]
+    for copy in (*firsts, *rows, *taken):
+        copy.start()
+    for copy in firsts:
+        copy.wait()
+    blocks = []
     lanes = out.shape[1]
     quarters = LAT // lanes
-    for k in range(quarters):
-        at = pl.multiple_of((step * quarters + k) * heads, heads)
-        held[pl.ds(at, heads), :] = latents[:, k * lanes : (k + 1) * lanes].astype(BF16)
-
-    @pl.when(step == n - 1)
-    def _():
-        rows, source = out.shape[0], held.shape[0]
-        slots = 2 * 4
-
-        def hit(o, c):
-            owner, i = o // slots, o % slots
-            want = i * (quarters * heads) + (owner % quarters) * heads + owner // quarters
-            return (i < slots // 2) & (c == want)
-
-        packed = dot(one_hot((rows, source), hit), held[...])
-        i = index(packed.shape, 0) % slots
-        for r in range(slots // 2):
-            packed = jnp.where(i == slots // 2 + r, ids[r].astype(F32), packed)
-        out[...] = packed.astype(BF16)
-
-
-def attend(query, cache_t, lengths, ids, owners):
+    for r in range(n):
+        rows[r].wait()
+        scores = dot(query_here[r], cache_here[r]) * SOFTMAX_SCALE
+        valid = index(scores.shape, 1) < lengths_here[r]
+        scores = jnp.where(valid, scores, -1e30)
+        raised = jnp.exp(scores - jnp.max(scores, axis=1, keepdims=True))
+        chances = (raised / jnp.sum(raised, axis=1, keepdims=True)).astype(BF16)
+        latents = dot_t(chances, cache_here[r, :LAT, :]).astype(BF16)
+        blocks += [latents[:, k * lanes : (k + 1) * lanes] for k in range(quarters)]
+        if r == n - 2:
+            for back, copy in zip(taken, given):
+                back.wait()
+                copy.start()
+    held = jnp.concatenate(blocks, axis=0)
+
+    def hit(o, c):
+        owner, i = o // (2 * n), o % (2 * n)
+        want = i * (quarters * heads) + (owner % quarters) * heads + owner // quarters
+        return (i < n) & (c == want)
+
+    packed = dot(one_hot((out.shape[0], held.shape[0]), hit), held)
+    i = index(packed.shape, 0) % (2 * n)
+    for r in range(n):
+        packed = jnp.where(i == n + r, ids_here[r].astype(F32), packed)
+    out[...] = packed.astype(BF16)
+    for copy in given:
+        copy.wait()
+
+
+def attend(query, cache_t, lengths, ids, weights, owners):
     n, heads, width = query.shape
     context = cache_t.shape[2]
     lanes = heads * LAT // owners
+    joined = (3, *weights[0].shape)
     return pl.pallas_call(
         attend_kernel,
-        out_shape=shape((owners * 2 * n, lanes), BF16),
-        grid_spec=pltpu.PrefetchScalarGridSpec(
-            num_scalar_prefetch=2,
-            grid=(n,),
-            in_specs=[
-                pl.BlockSpec((1, heads, width), lambda i, *_: (i, 0, 0)),
-                pl.BlockSpec((1, width, context), lambda i, *_: (i, 0, 0)),
-            ],
-            out_specs=pl.BlockSpec((owners * 2 * n, lanes), lambda i, *_: (0, 0)),
-            scratch_shapes=[pltpu.VMEM((n * heads * LAT // lanes, lanes), BF16)],
-        ),
+        out_shape=(shape((owners * 2 * n, lanes), BF16), shape(joined, BF16)),
+        in_specs=[FAR] * 7,
+        out_specs=(WHOLE, FAR),
+        scratch_shapes=[
+            pltpu.SMEM((n,), jnp.int32),
+            pltpu.SMEM((n,), jnp.int32),
+            pltpu.VMEM(query.shape, BF16),
+            pltpu.VMEM(cache_t.shape, BF16),
+            pltpu.VMEM(joined, BF16),
+            pltpu.SemaphoreType.DMA((3,)),
+            pltpu.SemaphoreType.DMA((n,)),
+            pltpu.SemaphoreType.DMA((6,)),
+        ],
         cost_estimate=pl.CostEstimate(
             flops=4 * n * heads * width * context,
             bytes_accessed=2 * n * width * context,
             transcendentals=0,
         ),
-        compiler_params=pltpu.CompilerParams(vmem_limit_bytes=53 * 2**20),
-    )(lengths, ids, query, cache_t)
+        compiler_params=pltpu.CompilerParams(vmem_limit_bytes=56 * 2**20),
+    )(lengths, ids, query, cache_t, *weights)
 
 
 def lora_kernel(arrived, down, copies, pieces, numbers):
@@ -217,15 +244,15 @@
     out[...] = total.astype(BF16)
 
 
-def ffn_kernel(rows, gate, up, down, out, gate_here, up_here, down_here, done):
+def ffn_kernel(rows, weights, out, gate_here, up_here, down_here, done):
     length, columns = rows.shape
     slots = length // CUTS
-    parts = [slice(at, at + columns) for at in range(0, gate.shape[1], columns)]
-    pairs = ((gate, gate_here), (up, up_here), (down, down_here))
+    parts = [slice(at, at + columns) for at in range(0, gate_here.shape[1], columns)]
+    here = (gate_here, up_here, down_here)
     fetches = [
         [
-            pltpu.make_async_copy(source.at[:, part], target.at[:, part], done.at[k, n])
-            for k, (source, target) in enumerate(pairs)
+            pltpu.make_async_copy(weights.at[k, :, part], here[k].at[:, part], done.at[k, n])
+            for k in range(3)
         ]
         for n, part in enumerate(parts)
     ]
@@ -255,13 +282,13 @@
     out[...] = dot(joint, stacked).astype(BF16)
 
 
-def ffn(rows, gate, up, down):
-    width, hidden = gate.shape
+def ffn(rows, weights):
+    _, width, hidden = weights.shape
     slots, columns = rows.shape[0] // CUTS, rows.shape[1]
     return pl.pallas_call(
         ffn_kernel,
         out_shape=shape(rows.shape, BF16),
-        in_specs=[WHOLE] + [pl.BlockSpec(memory_space=pl.ANY)] * 3,
+        in_specs=[WHOLE, FAR],
         out_specs=WHOLE,
         scratch_shapes=[pltpu.VMEM((width, hidden), BF16)] * 3
         + [pltpu.SemaphoreType.DMA((3, hidden // columns))],
@@ -270,8 +297,8 @@
             bytes_accessed=6 * width * hidden,
             transcendentals=0,
         ),
-        compiler_params=pltpu.CompilerParams(vmem_limit_bytes=50 * 2**20),
-    )(rows, gate, up, down)
+        compiler_params=pltpu.CompilerParams(vmem_limit_bytes=48 * 2**20),
+    )(rows, weights)
 
 
 def final_kernel(arrived, stream, out):
@@ -304,7 +331,14 @@
     columns = model_width // CUTS
     group = owners * requests
     owned_count = adapter_up_factors.shape[0] // RANK
-    packed = attend(q_latent, jnp.swapaxes(latent_cache, 1, 2), lengths, adapter_ids, owners)
+    packed, joined = attend(
+        q_latent,
+        jnp.swapaxes(latent_cache, 1, 2),
+        lengths,
+        adapter_ids,
+        (w_gate[0], w_up[0], w_down[0]),
+        owners,
+    )
     lanes = packed.shape[1]
     first = (lax.axis_index(EXPERT) * owned_count).astype(jnp.int32).reshape(1)
     packed, first = lax.optimization_barrier((packed, first))
@@ -363,9 +397,9 @@
     outgoing = call(pick_kernel, shape((long, columns), BF16))(
         in_specs=[WHOLE, WHOLE], out_specs=WHOLE
     )(pick, column)
-    gathered = [lax.all_gather(w[0], "dp", axis=1, tiled=True) for w in (w_gate, w_up, w_down)]
+    gathered = lax.all_gather(joined, "dp", axis=2, tiled=True)
     own_share = exchange(outgoing.reshape(experts, CUTS, columns), EXPERT).reshape(long, columns)
-    result = ffn(own_share, *gathered)
+    result = ffn(own_share, gathered)
     returned = exchange(result.reshape(experts, CUTS, columns), EXPERT).reshape(long, columns)
     routed = call(give_kernel, shape((wide, columns), BF16))(
         in_specs=[WHOLE, WHOLE], out_specs=WHOLE

time: 197 us -> 173 us (0.88)
  waiting for transfers between devices: 35.2 us -> 20.4 us
  blocking collectives: 122 us -> 114 us
  local copies, waits for them, and re-layouts: 3.02 us -> 0.83 us
    all_gather x3 -> x1, waiting for transfers between devices: 12.8 us -> 0.01 us  [local(): gathered = lax.all_gather(joined, 'dp', axis=2, tiled=True)]
    all_to_all x7, blocking collectives: 122 us -> 114 us  [exchange(): return lax.all_to_all(rows, axis, split_axis=0, concat_axis=0, tiled=True)]
    unnamed x21 -> x15, local copies, waits for them, and re-layouts: 2.3 us -> 0.12 us
    unnamed x3 -> x1, waiting for transfers between devices: 2.09 us -> 0.02 us
  transfers between devices with their start and end apart: 4 -> 2, of which waited for: 2 -> 1; matrix products, arithmetic and copies ran while one was open for 1% -> 1% of each run, Pallas kernels for 5% -> 2%
where the time goes in v3:
time: 173 us
  blocking collectives  114 us (66%)
  waiting for transfers between devices  20.4 us (12%)
  Pallas kernels  17.8 us (10%)
  between operations  13.6 us (8%)
  starting transfers between devices  4.65 us (3%)
    all_to_all x7, blocking collectives, exchange(): return lax.all_to_all(rows, axis, split_axis=0, concat_axis=0, tiled=True)  114 us
    all_to_all x1, waiting for transfers between devices, exchange(): return lax.all_to_all(rows, axis, split_axis=0, concat_axis=0, tiled=True)  20.4 us
    pallas_call x1, Pallas kernels, ffn(): pl.pallas_call(ffn_kernel, out_shape=shape(rows.shape, BF16), in_specs=[W...  7.07 us
    pallas_call x1, Pallas kernels, attend(): pl.pallas_call(attend_kernel, out_shape=(shape((owners * 2 * n, lanes), B...  5.48 us
    all_to_all x1, starting transfers between devices, exchange(): return lax.all_to_all(rows, axis, split_axis=0, concat_axis=0, tiled=True)  4.65 us
  transfers between devices with their start and end apart: 2, of which 1 were waited for; matrix products, arithmetic and copies ran while one was open for 1% of the time, Pallas kernels for 2%

profile of v3, /device:TPU:1, one launch (start us, length us, event | category | flops | bytes accessed | tf_op | source)
XLA Modules:
  0.0 172.6 jit_solution(10384076532074205735)
XLA Ops:
  6.5 0.0 all-gather.2.cloned.1.call-start
  6.5 0.0 copy-start
  6.5 5.5 %shard_map.136 = (bf16[512,128]{1,0:T(8,128)(2,1)}, bf16[3,2048,128]{2,1,0:T(8,128)(2,1)}) custom-call(s32[4]{0:T(128)} %lengths.1, s32[4]{0:T(128)} %ids.1, bf16[4,16,576]{2,1,0:T(8,128)(2,1)} %query.1, bf16[4,576,512]{2,1,0:T(8,128)(2,1)} %bitcast.40, bf16[2048,128]{1,0:T(8,128)(2,1)} %bitcast.41, bf16[2048,128]{1,0:T(8,128)(2,1)} %bitcast.42, ...), custom_call_target="tpu_custom_call" | custom-call | flops 75497472 | bytes 2359296 | tf_op jit(solution)/shard_map/pallas_call | solution.py:121
  12.0 0.0 copy-start.1
  12.0 0.0 copy-start.2
  12.1 0.0 all-gather.2.cloned.1.call-update
  12.1 28.8 %all_to_all.40 = bf16[64,8,128]{2,1,0:T(8,128)(2,1)S(1)} all-to-all(bf16[64,8,128]{2,1,0:T(8,128)(2,1)} %bitcast.44), channel_id=1, replica_groups=mesh['dp'=8,'expert_0'=8,'expert_1'=8] {'expert_0','expert_1'}, dimensions={0} | all-to-all | bytes 262144 | tf_op jit(solution)/shard_map/all_to_all | solution.py:42
  40.8 0.0 copy-done
  40.9 0.9 shard_map.137
  41.8 0.0 copy-start.3
  41.8 10.5 %all_to_all.41.arrived = f32[8,16,256]{2,1,0:T(8,128)S(1)} all-to-all(f32[8,16,256]{2,1,0:T(8,128)S(1)} %get-tuple-element.24), channel_id=1, replica_groups=mesh['dp'=8,'expert_0'=8,'expert_1'=8] {'expert_0'}, dimensions={0} | all-to-all | bytes 262144 | tf_op jit(solution)/shard_map/all_to_all | solution.py:42
  52.3 10.4 %all_to_all.42.arrived = f32[8,16,256]{2,1,0:T(8,128)S(1)} all-to-all(f32[8,16,256]{2,1,0:T(8,128)S(1)} %shard_map.138), channel_id=1, replica_groups=mesh['dp'=8,'expert_0'=8,'expert_1'=8] {'expert_1'}, dimensions={0} | all-to-all | bytes 262144 | tf_op jit(solution)/shard_map/all_to_all | solution.py:42
  62.8 0.0 copy-start.5
  62.8 0.0 copy-start.4
  62.8 0.0 copy-done.1
  62.8 0.0 copy-done.2
  62.8 0.0 copy-start.6
  62.8 1.7 %shard_map.139 = bf16[64,32,256]{2,1,0:T(8,128)(2,1)} custom-call(s32[1]{0:T(128)} %bitcast.4.first, f32[8,16,256]{2,1,0:T(8,128)S(1)} %all_to_all.42.arrived, bf16[256,128]{1,0:T(8,128)(2,1)S(1)} %get-tuple-element.25.pieces, f32[8,256]{1,0:T(8,128)S(1)} %get-tuple-element.26.numbers, bf16[128,2048]{1,0:T(8,128)(2,1)S(1)} %copy-done.1, ...), custom_call_target="tpu_custom_call" | custom-call | flops 10000000 | bytes 1000000 | tf_op jit(solution)/shard_map/pallas_call | solution.py:361
  64.5 4.7 %all-to-all-start.3 = ((bf16[64,32,256]{2,1,0:T(8,128)(2,1)}), bf16[64,32,256]{2,1,0:T(8,128)(2,1)S(1)}, u32[]{:S(2)}, u32[]{:S(2)}) async-start(bf16[64,32,256]{2,1,0:T(8,128)(2,1)} %shard_map.139), calls=%async_computation.3 | async-start | bytes 2097152 | tf_op jit(solution)/shard_map/all_to_all | solution.py:42
  69.2 0.0 copy-done.3
  69.2 0.1 copy.31
  69.3 0.1 eq.45
  69.4 0.6 reduce-window.6
  70.0 0.2 slice_reduce_fusion
  70.3 0.1 bitcast_bitcast_fusion
  70.4 0.1 eq.54
  70.5 0.1 copy.34
  70.6 0.1 fusion.1
  70.8 0.1 copy.35
  70.9 0.0 copy-done.5
  70.9 0.1 select_reduce_fusion
  71.0 0.1 copy.36
  71.1 0.0 copy-done.4
  71.1 0.0 copy-done.6
  71.2 0.8 shard_map.140
  72.0 20.4 %all-to-all-done.3.arrived = bf16[64,32,256]{2,1,0:T(8,128)(2,1)S(1)} async-done(((bf16[64,32,256]{2,1,0:T(8,128)(2,1)}), bf16[64,32,256]{2,1,0:T(8,128)(2,1)S(1)}, u32[]{:S(2)}, u32[]{:S(2)}) %all-to-all-start.3) | async-done | bytes 1048608 | tf_op jit(solution)/shard_map/all_to_all | solution.py:42
  92.4 0.5 shard_map.141
  92.9 16.7 %all_to_all.43 = bf16[8,32,256]{2,1,0:T(8,128)(2,1)S(1)} all-to-all(bf16[8,32,256]{2,1,0:T(8,128)(2,1)S(1)} %get-tuple-element.34), channel_id=1, replica_groups=mesh['dp'=8,'expert_0'=8,'expert_1'=8] {'dp'}, dimensions={0} | all-to-all | bytes 262144 | tf_op jit(solution)/shard_map/all_to_all | solution.py:42
  109.6 0.2 shard_map.142
  109.9 18.3 %all_to_all.44 = bf16[64,8,256]{2,1,0:T(8,128)(2,1)S(1)} all-to-all(bf16[64,8,256]{2,1,0:T(8,128)(2,1)S(1)} %bitcast.33), channel_id=1, replica_groups=mesh['dp'=8,'expert_0'=8,'expert_1'=8] {'expert_0','expert_1'}, dimensions={0} | all-to-all | bytes 524288 | tf_op jit(solution)/shard_map/all_to_all | solution.py:42
  128.2 0.0 all-gather.2.cloned.1.call-done.weights
  128.2 7.1 %shard_map.143 = bf16[512,256]{1,0:T(8,128)(2,1)S(1)} custom-call(bf16[512,256]{1,0:T(8,128)(2,1)S(1)} %bitcast.31, bf16[3,2048,1024]{2,1,0:T(8,128)(2,1)} %all-gather.2.cloned.1.call-done.weights), custom_call_target="tpu_custom_call" | custom-call | flops 805306368 | bytes 12582912 | tf_op jit(solution)/shard_map/pallas_call | solution.py:288
  135.3 18.3 %all_to_all.45 = bf16[64,8,256]{2,1,0:T(8,128)(2,1)S(1)} all-to-all(bf16[64,8,256]{2,1,0:T(8,128)(2,1)S(1)} %bitcast.32), channel_id=1, replica_groups=mesh['dp'=8,'expert_0'=8,'expert_1'=8] {'expert_0','expert_1'}, dimensions={0} | all-to-all | bytes 524288 | tf_op jit(solution)/shard_map/all_to_all | solution.py:42
  153.5 0.4 shard_map.144
  154.0 11.1 %all_to_all.46.arrived = bf16[8,32,256]{2,1,0:T(8,128)(2,1)S(1)} all-to-all(bf16[8,32,256]{2,1,0:T(8,128)(2,1)S(1)} %bitcast.37), channel_id=1, replica_groups=mesh['dp'=8,'expert_0'=8,'expert_1'=8] {'dp'}, dimensions={0} | all-to-all | bytes 262144 | tf_op jit(solution)/shard_map/all_to_all | solution.py:42
  165.1 0.6 shard_map.145
  (13 shorter events, 0.2 us)
Async XLA Ops:
  6.5 121.7 %all-gather.2.cloned.1.call-start = ((), (), s32[]{:S(2)}) async-start(), calls=%async_computation.8 | async-start | bytes 14155776 | tf_op jit(solution)/shard_map/all_gather | solution.py:400
  6.5 34.3 %copy-start = (bf16[128,2048]{1,0:T(8,128)(2,1)S(1)}, bf16[128,2048]{1,0:T(8,128)(2,1)}, u32[]{:S(2)}) copy-start(bf16[128,2048]{1,0:T(8,128)(2,1)} %down.1) | copy-start | bytes 1572868
  12.0 50.7 %copy-start.1 = (bf16[128,2048]{1,0:T(8,128)(2,1)S(1)}, bf16[128,2048]{1,0:T(8,128)(2,1)}, u32[]{:S(2)}) copy-start(bf16[128,2048]{1,0:T(8,128)(2,1)} %value.1) | copy-start | bytes 1572868
  12.0 50.7 %copy-start.2 = (bf16[32,2048]{1,0:T(8,128)(2,1)S(1)}, bf16[32,2048]{1,0:T(8,128)(2,1)}, u32[]{:S(2)}) copy-start(bf16[32,2048]{1,0:T(8,128)(2,1)} %up.1) | copy-start | bytes 393220
  41.8 27.4 %copy-start.3 = (s32[32,6]{0,1:T(8,128)S(1)}, s32[32,6]{0,1:T(8,128)}, u32[]{:S(2)}) copy-start(s32[32,6]{0,1:T(8,128)} %param.23) | copy-start | bytes 2308
  62.8 8.1 %copy-start.5 = (f32[32,6]{0,1:T(8,128)S(1)}, f32[32,6]{0,1:T(8,128)}, u32[]{:S(2)}) copy-start(f32[32,6]{0,1:T(8,128)} %param.24) | copy-start | bytes 2308
  62.8 8.4 %copy-start.4 = (bf16[4,2048]{1,0:T(4,128)(2,1)S(1)}, bf16[4,2048]{1,0:T(4,128)(2,1)}, u32[]{:S(2)}) copy-start(bf16[4,2048]{1,0:T(4,128)(2,1)} %param.17) | copy-start | bytes 49156
  62.8 8.4 %copy-start.6 = (bf16[2048]{0:T(1024)(128)(2,1)S(1)}, bf16[2048]{0:T(1024)(128)(2,1)}, u32[]{:S(2)}) copy-start(bf16[2048]{0:T(1024)(128)(2,1)} %param.22) | copy-start | bytes 12292
  64.5 27.9 %all-to-all-start.3 = ((bf16[64,32,256]{2,1,0:T(8,128)(2,1)}), bf16[64,32,256]{2,1,0:T(8,128)(2,1)S(1)}, u32[]{:S(2)}, u32[]{:S(2)}) async-start(bf16[64,32,256]{2,1,0:T(8,128)(2,1)} %shard_map.139), calls=%async_computation.3 | async-start | bytes 2097152 | tf_op jit(solution)/shard_map/all_to_all | solution.py:42
Sparse Core Ops, SparseCore 0:
  12.2 82.7 all-gather.1

commit v4 on v3

--- a/solution.py
+++ b/solution.py
@@ -244,18 +244,27 @@
     out[...] = total.astype(BF16)
 
 
-def ffn_kernel(rows, weights, out, gate_here, up_here, down_here, done):
+def ffn_kernel(rows, *rest):
+    shards, (out, gate, up, down, done) = rest[:-5], rest[-5:]
     length, columns = rows.shape
     slots = length // CUTS
-    parts = [slice(at, at + columns) for at in range(0, gate_here.shape[1], columns)]
-    here = (gate_here, up_here, down_here)
-    fetches = [
-        [
-            pltpu.make_async_copy(weights.at[k, :, part], here[k].at[:, part], done.at[k, n])
-            for k in range(3)
-        ]
-        for n, part in enumerate(parts)
-    ]
+    shards = [(w, (i,)) for w in shards for i in range(w.shape[0])]
+    lanes = shards[0][0].shape[-1]
+    per = gate.shape[2] // lanes
+    fetches = []
+    for n in range(gate.shape[0]):
+        fetch = []
+        for k, here in enumerate((gate, up, down)):
+            for i in range(per):
+                source, at = shards[n * per + i]
+                fetch.append(
+                    pltpu.make_async_copy(
+                        source.at[(*at, k)],
+                        here.at[n, :, i * lanes : (i + 1) * lanes],
+                        done.at[n, k * per + i],
+                    )
+                )
+        fetches.append(fetch)
     for fetch in fetches:
         for copy in fetch:
             copy.start()
@@ -265,14 +274,17 @@
         [apart[cut * slots : (cut + 1) * slots] for cut in range(CUTS)], axis=1
     )
     total = None
-    for part, fetch in zip(parts, fetches):
-        fetch[0].wait()
-        gated = dot(tokens, gate_here[:, part])
-        fetch[1].wait()
-        raised = dot(tokens, up_here[:, part])
+    for n, fetch in enumerate(fetches):
+        for copy in fetch[:per]:
+            copy.wait()
+        gated = dot(tokens, gate[n])
+        for copy in fetch[per : 2 * per]:
+            copy.wait()
+        raised = dot(tokens, up[n])
         acted = (gated / (1.0 + jnp.exp(-gated)) * raised).astype(BF16)
-        fetch[2].wait()
-        term = dot_t(acted, down_here[:, part])
+        for copy in fetch[2 * per :]:
+            copy.wait()
+        term = dot_t(acted, down[n])
         total = term if total is None else total + term
     result = total.astype(BF16)
     stacked = jnp.concatenate(
@@ -282,23 +294,26 @@
     out[...] = dot(joint, stacked).astype(BF16)
 
 
-def ffn(rows, weights):
-    _, width, hidden = weights.shape
-    slots, columns = rows.shape[0] // CUTS, rows.shape[1]
+def ffn(rows, *weights):
+    _, kinds, width, lanes = weights[0].shape
+    hidden = lanes * sum(w.shape[0] for w in weights)
+    slots = rows.shape[0] // CUTS
+    per = 2
+    chunk = pltpu.VMEM((hidden // (per * lanes), width, per * lanes), BF16)
     return pl.pallas_call(
         ffn_kernel,
         out_shape=shape(rows.shape, BF16),
-        in_specs=[WHOLE, FAR],
+        in_specs=[WHOLE] + [FAR] * len(weights),
         out_specs=WHOLE,
-        scratch_shapes=[pltpu.VMEM((width, hidden), BF16)] * 3
-        + [pltpu.SemaphoreType.DMA((3, hidden // columns))],
+        scratch_shapes=[chunk] * 3
+        + [pltpu.SemaphoreType.DMA((hidden // (per * lanes), kinds * per))],
         cost_estimate=pl.CostEstimate(
             flops=6 * slots * width * hidden,
             bytes_accessed=6 * width * hidden,
             transcendentals=0,
         ),
         compiler_params=pltpu.CompilerParams(vmem_limit_bytes=48 * 2**20),
-    )(rows, weights)
+    )(rows, *weights)
 
 
 def final_kernel(arrived, stream, out):
@@ -397,7 +412,7 @@
     outgoing = call(pick_kernel, shape((long, columns), BF16))(
         in_specs=[WHOLE, WHOLE], out_specs=WHOLE
     )(pick, column)
-    gathered = lax.all_gather(joined, "dp", axis=2, tiled=True)
+    gathered = lax.all_gather(joined, "dp", axis=0)
     own_share = exchange(outgoing.reshape(experts, CUTS, columns), EXPERT).reshape(long, columns)
     result = ffn(own_share, gathered)
     returned = exchange(result.reshape(experts, CUTS, columns), EXPERT).reshape(long, columns)

time: 173 us -> 173 us (level)
  no operation moved by 1% of the time
where the time goes in v4:
time: 173 us
  blocking collectives  114 us (66%)
  waiting for transfers between devices  20.4 us (12%)
  Pallas kernels  17.8 us (10%)
  between operations  13.6 us (8%)
  starting transfers between devices  4.65 us (3%)
    all_to_all x7, blocking collectives, exchange(): return lax.all_to_all(rows, axis, split_axis=0, concat_axis=0, tiled=True)  114 us
    all_to_all x1, waiting for transfers between devices, exchange(): return lax.all_to_all(rows, axis, split_axis=0, concat_axis=0, tiled=True)  20.4 us
    pallas_call x1, Pallas kernels, ffn(): pl.pallas_call(ffn_kernel, out_shape=shape(rows.shape, BF16), in_specs=[W...  7.08 us
    pallas_call x1, Pallas kernels, attend(): pl.pallas_call(attend_kernel, out_shape=(shape((owners * 2 * n, lanes), B...  5.48 us
    all_to_all x1, starting transfers between devices, exchange(): return lax.all_to_all(rows, axis, split_axis=0, concat_axis=0, tiled=True)  4.65 us
  transfers between devices with their start and end apart: 2, of which 1 were waited for; matrix products, arithmetic and copies ran while one was open for 1% of the time, Pallas kernels for 2%

profile of v4, /device:TPU:1, one launch (start us, length us, event | category | flops | bytes accessed | tf_op | source)
XLA Modules:
  0.0 172.6 jit_solution(9564691880956144027)
XLA Ops:
  6.5 0.0 all-gather.3.cloned.1.call-start
  6.5 0.0 copy-start
  6.5 5.5 %shard_map.136 = (bf16[512,128]{1,0:T(8,128)(2,1)}, bf16[3,2048,128]{2,1,0:T(8,128)(2,1)}) custom-call(s32[4]{0:T(128)} %lengths.1, s32[4]{0:T(128)} %ids.1, bf16[4,16,576]{2,1,0:T(8,128)(2,1)} %query.1, bf16[4,576,512]{2,1,0:T(8,128)(2,1)} %bitcast.42, bf16[2048,128]{1,0:T(8,128)(2,1)} %bitcast.43, bf16[2048,128]{1,0:T(8,128)(2,1)} %bitcast.44, ...), custom_call_target="tpu_custom_call" | custom-call | flops 75497472 | bytes 2359296 | tf_op jit(solution)/shard_map/pallas_call | solution.py:121
  12.0 0.0 copy-start.1
  12.0 0.0 copy-start.2
  12.1 0.0 all-gather.3.cloned.1.call-update
  12.1 28.8 %all_to_all.40 = bf16[64,8,128]{2,1,0:T(8,128)(2,1)S(1)} all-to-all(bf16[64,8,128]{2,1,0:T(8,128)(2,1)} %bitcast.46), channel_id=1, replica_groups=mesh['dp'=8,'expert_0'=8,'expert_1'=8] {'expert_0','expert_1'}, dimensions={0} | all-to-all | bytes 262144 | tf_op jit(solution)/shard_map/all_to_all | solution.py:42
  40.8 0.0 copy-done
  40.9 0.9 shard_map.137
  41.8 0.0 copy-start.3
  41.8 10.5 %all_to_all.41.arrived = f32[8,16,256]{2,1,0:T(8,128)S(1)} all-to-all(f32[8,16,256]{2,1,0:T(8,128)S(1)} %get-tuple-element.24), channel_id=1, replica_groups=mesh['dp'=8,'expert_0'=8,'expert_1'=8] {'expert_0'}, dimensions={0} | all-to-all | bytes 262144 | tf_op jit(solution)/shard_map/all_to_all | solution.py:42
  52.3 10.4 %all_to_all.42.arrived = f32[8,16,256]{2,1,0:T(8,128)S(1)} all-to-all(f32[8,16,256]{2,1,0:T(8,128)S(1)} %shard_map.138), channel_id=1, replica_groups=mesh['dp'=8,'expert_0'=8,'expert_1'=8] {'expert_1'}, dimensions={0} | all-to-all | bytes 262144 | tf_op jit(solution)/shard_map/all_to_all | solution.py:42
  62.8 0.0 copy-start.5
  62.8 0.0 copy-start.4
  62.8 0.0 copy-done.1
  62.8 0.0 copy-done.2
  62.8 0.0 copy-start.6
  62.8 1.7 %shard_map.139 = bf16[64,32,256]{2,1,0:T(8,128)(2,1)} custom-call(s32[1]{0:T(128)} %bitcast.4.first, f32[8,16,256]{2,1,0:T(8,128)S(1)} %all_to_all.42.arrived, bf16[256,128]{1,0:T(8,128)(2,1)S(1)} %get-tuple-element.25.pieces, f32[8,256]{1,0:T(8,128)S(1)} %get-tuple-element.26.numbers, bf16[128,2048]{1,0:T(8,128)(2,1)S(1)} %copy-done.1, ...), custom_call_target="tpu_custom_call" | custom-call | flops 10000000 | bytes 1000000 | tf_op jit(solution)/shard_map/pallas_call | solution.py:376
  64.5 4.7 %all-to-all-start.3 = ((bf16[64,32,256]{2,1,0:T(8,128)(2,1)}), bf16[64,32,256]{2,1,0:T(8,128)(2,1)S(1)}, u32[]{:S(2)}, u32[]{:S(2)}) async-start(bf16[64,32,256]{2,1,0:T(8,128)(2,1)} %shard_map.139), calls=%async_computation.3 | async-start | bytes 2097152 | tf_op jit(solution)/shard_map/all_to_all | solution.py:42
  69.2 0.0 copy-done.3
  69.2 0.1 copy.37
  69.3 0.1 eq.45
  69.4 0.6 reduce-window.6
  70.0 0.2 slice_reduce_fusion
  70.3 0.1 bitcast_bitcast_fusion
  70.4 0.1 eq.54
  70.5 0.1 copy.40
  70.6 0.1 fusion.1
  70.8 0.1 copy.41
  70.9 0.0 copy-done.5
  70.9 0.1 select_reduce_fusion
  71.0 0.1 copy.42
  71.1 0.0 copy-done.4
  71.1 0.0 copy-done.6
  71.2 0.8 shard_map.140
  72.0 20.4 %all-to-all-done.3.arrived = bf16[64,32,256]{2,1,0:T(8,128)(2,1)S(1)} async-done(((bf16[64,32,256]{2,1,0:T(8,128)(2,1)}), bf16[64,32,256]{2,1,0:T(8,128)(2,1)S(1)}, u32[]{:S(2)}, u32[]{:S(2)}) %all-to-all-start.3) | async-done | bytes 1048608 | tf_op jit(solution)/shard_map/all_to_all | solution.py:42
  92.4 0.5 shard_map.141
  92.9 16.7 %all_to_all.43 = bf16[8,32,256]{2,1,0:T(8,128)(2,1)S(1)} all-to-all(bf16[8,32,256]{2,1,0:T(8,128)(2,1)S(1)} %get-tuple-element.34), channel_id=1, replica_groups=mesh['dp'=8,'expert_0'=8,'expert_1'=8] {'dp'}, dimensions={0} | all-to-all | bytes 262144 | tf_op jit(solution)/shard_map/all_to_all | solution.py:42
  109.6 0.2 shard_map.142
  109.9 18.3 %all_to_all.44 = bf16[64,8,256]{2,1,0:T(8,128)(2,1)S(1)} all-to-all(bf16[64,8,256]{2,1,0:T(8,128)(2,1)S(1)} %bitcast.34), channel_id=1, replica_groups=mesh['dp'=8,'expert_0'=8,'expert_1'=8] {'expert_0','expert_1'}, dimensions={0} | all-to-all | bytes 524288 | tf_op jit(solution)/shard_map/all_to_all | solution.py:42
  128.2 0.0 all-gather.3.cloned.1.call-done
  128.2 7.1 %shard_map.143 = bf16[512,256]{1,0:T(8,128)(2,1)S(1)} custom-call(bf16[512,256]{1,0:T(8,128)(2,1)S(1)} %bitcast.32, bf16[8,3,2048,128]{3,2,1,0:T(8,128)(2,1)} %bitcast.41), custom_call_target="tpu_custom_call" | custom-call | flops 805306368 | bytes 12582912 | tf_op jit(solution)/shard_map/pallas_call | solution.py:303
  135.3 18.3 %all_to_all.45 = bf16[64,8,256]{2,1,0:T(8,128)(2,1)S(1)} all-to-all(bf16[64,8,256]{2,1,0:T(8,128)(2,1)S(1)} %bitcast.33), channel_id=1, replica_groups=mesh['dp'=8,'expert_0'=8,'expert_1'=8] {'expert_0','expert_1'}, dimensions={0} | all-to-all | bytes 524288 | tf_op jit(solution)/shard_map/all_to_all | solution.py:42
  153.6 0.4 shard_map.144
  154.0 11.1 %all_to_all.46.arrived = bf16[8,32,256]{2,1,0:T(8,128)(2,1)S(1)} all-to-all(bf16[8,32,256]{2,1,0:T(8,128)(2,1)S(1)} %bitcast.38), channel_id=1, replica_groups=mesh['dp'=8,'expert_0'=8,'expert_1'=8] {'dp'}, dimensions={0} | all-to-all | bytes 262144 | tf_op jit(solution)/shard_map/all_to_all | solution.py:42
  165.1 0.6 shard_map.145
  (13 shorter events, 0.2 us)
Async XLA Ops:
  6.5 121.7 %all-gather.3.cloned.1.call-start = ((), (), s32[]{:S(2)}) async-start(), calls=%async_computation.8 | async-start | bytes 14155776 | tf_op jit(solution)/shard_map/all_gather | solution.py:415
  6.5 34.3 %copy-start = (bf16[128,2048]{1,0:T(8,128)(2,1)S(1)}, bf16[128,2048]{1,0:T(8,128)(2,1)}, u32[]{:S(2)}) copy-start(bf16[128,2048]{1,0:T(8,128)(2,1)} %down.1) | copy-start | bytes 1572868
  12.0 50.7 %copy-start.1 = (bf16[128,2048]{1,0:T(8,128)(2,1)S(1)}, bf16[128,2048]{1,0:T(8,128)(2,1)}, u32[]{:S(2)}) copy-start(bf16[128,2048]{1,0:T(8,128)(2,1)} %value.1) | copy-start | bytes 1572868
  12.0 50.7 %copy-start.2 = (bf16[32,2048]{1,0:T(8,128)(2,1)S(1)}, bf16[32,2048]{1,0:T(8,128)(2,1)}, u32[]{:S(2)}) copy-start(bf16[32,2048]{1,0:T(8,128)(2,1)} %up.1) | copy-start | bytes 393220
  41.8 27.4 %copy-start.3 = (s32[32,6]{0,1:T(8,128)S(1)}, s32[32,6]{0,1:T(8,128)}, u32[]{:S(2)}) copy-start(s32[32,6]{0,1:T(8,128)} %param.23) | copy-start | bytes 2308
  62.8 8.1 %copy-start.5 = (f32[32,6]{0,1:T(8,128)S(1)}, f32[32,6]{0,1:T(8,128)}, u32[]{:S(2)}) copy-start(f32[32,6]{0,1:T(8,128)} %param.24) | copy-start | bytes 2308
  62.8 8.4 %copy-start.4 = (bf16[4,2048]{1,0:T(4,128)(2,1)S(1)}, bf16[4,2048]{1,0:T(4,128)(2,1)}, u32[]{:S(2)}) copy-start(bf16[4,2048]{1,0:T(4,128)(2,1)} %param.17) | copy-start | bytes 49156
  62.8 8.4 %copy-start.6 = (bf16[2048]{0:T(1024)(128)(2,1)S(1)}, bf16[2048]{0:T(1024)(128)(2,1)}, u32[]{:S(2)}) copy-start(bf16[2048]{0:T(1024)(128)(2,1)} %param.22) | copy-start | bytes 12292
  64.5 27.9 %all-to-all-start.3 = ((bf16[64,32,256]{2,1,0:T(8,128)(2,1)}), bf16[64,32,256]{2,1,0:T(8,128)(2,1)S(1)}, u32[]{:S(2)}, u32[]{:S(2)}) async-start(bf16[64,32,256]{2,1,0:T(8,128)(2,1)} %shard_map.139), calls=%async_computation.3 | async-start | bytes 2097152 | tf_op jit(solution)/shard_map/all_to_all | solution.py:42
Sparse Core Ops, SparseCore 0:
  12.2 78.4 all-gather.2

commit v5 on v4

--- a/solution.py
+++ b/solution.py
@@ -36,6 +36,10 @@
         cost_estimate=pl.CostEstimate(flops=flops, bytes_accessed=nbytes, transcendentals=0),
         compiler_params=GRANT,
     )
+
+
+def moved(block, where):
+    return lax.ppermute(block, "dp", list(enumerate(where)))
 
 
 def exchange(rows, axis):
@@ -312,7 +316,7 @@
             bytes_accessed=6 * width * hidden,
             transcendentals=0,
         ),
-        compiler_params=pltpu.CompilerParams(vmem_limit_bytes=48 * 2**20),
+        compiler_params=pltpu.CompilerParams(vmem_limit_bytes=52 * 2**20),
     )(rows, *weights)
 
 
@@ -358,6 +362,21 @@
     first = (lax.axis_index(EXPERT) * owned_count).astype(jnp.int32).reshape(1)
     packed, first = lax.optimization_barrier((packed, first))
     arrived = exchange(packed.reshape(owners, 2 * requests, lanes), EXPERT)
+    ups = [(d + 2) % dp_count for d in range(dp_count)]
+    downs = [(d - 2) % dp_count for d in range(dp_count)]
+    swap = [d ^ 1 for d in range(dp_count)]
+    from_below = moved(joined, ups)
+    from_above = moved(joined, downs)
+    shards = [joined, from_below, from_above]
+    own_swapped = moved(joined, swap)
+    arrived, own_swapped = lax.optimization_barrier((arrived, own_swapped))
+    shards.append(own_swapped)
+    on = jnp.where(lax.axis_index("dp") % 2 == 0, from_above, from_below)
+    relayed = [downs[d] if d % 2 == 0 else ups[d] for d in range(dp_count)]
+    opposite = moved(on, relayed)
+    below_swapped = moved(from_below, swap)
+    above_swapped = moved(from_above, swap)
+    opposite_swapped = moved(opposite, swap)
     arrived = arrived.reshape(owners * 2 * requests, lanes)
     side = lax.axis_size(EXPERT[0])
     copies, pieces, numbers = call(
@@ -373,7 +392,7 @@
         in_specs=[WHOLE], out_specs=WHOLE
     )(half)
     summed = exchange(copies, EXPERT[1])
-    partial = call(project_kernel, shape((owners, CUTS * requests, columns), BF16))(
+    partial = call(project_kernel, pltpu.HBM((owners, CUTS * requests, columns), BF16))(
         in_specs=[SCALARS, WHOLE, WHOLE, WHOLE, WHOLE, WHOLE], out_specs=WHOLE
     )(first, summed, pieces, numbers, value_out, adapter_up_factors)
     at_home = exchange(partial, EXPERT)
@@ -401,20 +420,23 @@
     gain_cut = jnp.broadcast_to(
         cut_rows(norm_gain.astype(F32)), (CUTS, requests, columns)
     ).reshape(CUTS * requests, columns)
-    at_home, pick, give, residual_cut, gain_cut = lax.optimization_barrier(
-        (at_home, pick, give, residual_cut, gain_cut)
-    )
+    at_home, pick, give, residual_cut, gain_cut, below_swapped, above_swapped = (
+        lax.optimization_barrier(
+            (at_home, pick, give, residual_cut, gain_cut, below_swapped, above_swapped)
+        )
+    )
+    shards += [opposite, below_swapped, above_swapped, opposite_swapped]
     stream, copies = call(
         norm_kernel,
         (shape((CUTS * requests, columns), F32), shape((dp_count, CUTS * requests, columns), BF16)),
     )(in_specs=[WHOLE, WHOLE, WHOLE], out_specs=(WHOLE, WHOLE))(at_home, residual_cut, gain_cut)
     column = exchange(copies, "dp").reshape(wide, columns)
-    outgoing = call(pick_kernel, shape((long, columns), BF16))(
+    outgoing = call(pick_kernel, pltpu.HBM((long, columns), BF16))(
         in_specs=[WHOLE, WHOLE], out_specs=WHOLE
     )(pick, column)
-    gathered = lax.all_gather(joined, "dp", axis=0)
-    own_share = exchange(outgoing.reshape(experts, CUTS, columns), EXPERT).reshape(long, columns)
-    result = ffn(own_share, gathered)
+    own_share = exchange(outgoing.reshape(experts, CUTS, columns), EXPERT)
+    own_share = own_share.reshape(long, columns)
+    result = ffn(own_share, *(w[None] for w in shards))
     returned = exchange(result.reshape(experts, CUTS, columns), EXPERT).reshape(long, columns)
     routed = call(give_kernel, shape((wide, columns), BF16))(
         in_specs=[WHOLE, WHOLE], out_specs=WHOLE

time: 173 us -> 191 us (1.10)
  starting transfers between devices: 4.65 us -> 57.4 us
  blocking collectives: 114 us -> 79.2 us
  between operations: 13.6 us -> 0.34 us
  waiting for transfers between devices: 20.4 us -> 29.7 us
  other arithmetic: 1.1 us -> 3.83 us
    ppermute x0 -> x7, starting transfers between devices: none -> 35.6 us  [moved(): return lax.ppermute(block, 'dp', list(enumerate(where)))]
    all_to_all x7 -> x5, blocking collectives: 114 us -> 79.2 us  [exchange(): return lax.all_to_all(rows, axis, split_axis=0, concat_axis=0, tiled=True)]
    all_to_all x1 -> x3, starting transfers between devices: 4.65 us -> 21.9 us  [exchange(): return lax.all_to_all(rows, axis, split_axis=0, concat_axis=0, tiled=True)]
    ppermute x0 -> x7, waiting for transfers between devices: none -> 10.4 us  [moved(): return lax.ppermute(block, 'dp', list(enumerate(where)))]
    select_n x0 -> x1, other arithmetic: none -> 2.74 us  [local(): on = jnp.where(lax.axis_index('dp') % 2 == 0, from_above, from_below)]
    all_to_all x1 -> x3, waiting for transfers between devices: 20.4 us -> 19.3 us  [exchange(): return lax.all_to_all(rows, axis, split_axis=0, concat_axis=0, tiled=True)]
  transfers between devices with their start and end apart: 2 -> 10, of which waited for: 1 -> 4; matrix products, arithmetic and copies ran while one was open for 1% -> 2% of each run, Pallas kernels for 2% -> 3%
where the time goes in v5:
time: 191 us; the launch traced here: 190 us
  blocking collectives  79.2 us (41%)
  starting transfers between devices  57.4 us (30%)
  waiting for transfers between devices  29.7 us (16%)
  Pallas kernels  18.5 us (10%)
  other arithmetic  3.83 us (2%)
    all_to_all x5, blocking collectives, exchange(): return lax.all_to_all(rows, axis, split_axis=0, concat_axis=0, tiled=True)  79.2 us
    ppermute x7, starting transfers between devices, moved(): return lax.ppermute(block, 'dp', list(enumerate(where)))  35.6 us
    all_to_all x3, starting transfers between devices, exchange(): return lax.all_to_all(rows, axis, split_axis=0, concat_axis=0, tiled=True)  21.9 us
    all_to_all x3, waiting for transfers between devices, exchange(): return lax.all_to_all(rows, axis, split_axis=0, concat_axis=0, tiled=True)  19.3 us
    ppermute x7, waiting for transfers between devices, moved(): return lax.ppermute(block, 'dp', list(enumerate(where)))  10.4 us
    pallas_call x1, Pallas kernels, ffn(): pl.pallas_call(ffn_kernel, out_shape=shape(rows.shape, BF16), in_specs=[W...  7.08 us
    pallas_call x1, Pallas kernels, attend(): pl.pallas_call(attend_kernel, out_shape=(shape((owners * 2 * n, lanes), B...  5.38 us
  transfers between devices with their start and end apart: 10, of which 4 were waited for; matrix products, arithmetic and copies ran while one was open for 2% of the time, Pallas kernels for 3%

profile of v5, /device:TPU:1, one launch (start us, length us, event | category | flops | bytes accessed | tf_op | source)
XLA Modules:
  0.0 189.8 jit_solution(9882181056624632738)
XLA Ops:
  0.0 5.4 %shard_map.136 = (bf16[512,128]{1,0:T(8,128)(2,1)}, bf16[3,2048,128]{2,1,0:T(8,128)(2,1)}) custom-call(s32[4]{0:T(128)} %lengths.1, s32[4]{0:T(128)} %ids.1, bf16[4,16,576]{2,1,0:T(8,128)(2,1)} %query.1, bf16[4,576,512]{2,1,0:T(8,128)(2,1)} %bitcast.47, bf16[2048,128]{1,0:T(8,128)(2,1)} %bitcast.51, bf16[2048,128]{1,0:T(8,128)(2,1)} %bitcast.52, ...), custom_call_target="tpu_custom_call" | custom-call | flops 75497472 | bytes 2359296 | tf_op jit(solution)/shard_map/pallas_call | solution.py:125
  5.4 3.9 %collective-permute-start.1 = (bf16[3,2048,128]{2,1,0:T(8,128)(2,1)}, bf16[3,2048,128]{2,1,0:T(8,128)(2,1)}, u32[]{:S(2)}, u32[]{:S(2)}) collective-permute-start(bf16[3,2048,128]{2,1,0:T(8,128)(2,1)} %get-tuple-element.28), channel_id=1, source_target_pairs={{0,128},{64,192},{128,256},{192,320},{256,384},{320,448},{384,0},{... | collective-permute-start | bytes 4718600 | tf_op jit(solution)/shard_map/ppermute | solution.py:42
  9.3 3.2 %collective-permute-start.3 = (bf16[3,2048,128]{2,1,0:T(8,128)(2,1)}, bf16[3,2048,128]{2,1,0:T(8,128)(2,1)}, u32[]{:S(2)}, u32[]{:S(2)}) collective-permute-start(bf16[3,2048,128]{2,1,0:T(8,128)(2,1)} %get-tuple-element.28), channel_id=1, source_target_pairs={{0,384},{64,448},{128,0},{192,64},{256,128},{320,192},{384,256},{4... | collective-permute-start | bytes 4718600 | tf_op jit(solution)/shard_map/ppermute | solution.py:42
  12.5 8.7 %collective-permute-start = (bf16[3,2048,128]{2,1,0:T(8,128)(2,1)}, bf16[3,2048,128]{2,1,0:T(8,128)(2,1)S(1)}, u32[]{:S(2)}, u32[]{:S(2)}) collective-permute-start(bf16[3,2048,128]{2,1,0:T(8,128)(2,1)} %get-tuple-element.28), channel_id=1, source_target_pairs={{0,64},{64,0},{128,192},{192,128},{256,320},{320,256},{384,448},{4... | collective-permute-start | bytes 4718600 | tf_op jit(solution)/shard_map/ppermute | solution.py:42
  21.2 11.0 %all-to-all-start = ((bf16[64,8,128]{2,1,0:T(8,128)(2,1)}), bf16[64,8,128]{2,1,0:T(8,128)(2,1)S(1)}, u32[]{:S(2)}, u32[]{:S(2)}) async-start(bf16[64,8,128]{2,1,0:T(8,128)(2,1)} %bitcast.54), calls=%async_computation | async-start | bytes 262144 | tf_op jit(solution)/shard_map/all_to_all | solution.py:46
  32.2 0.0 copy-start
  32.2 0.0 copy-start.2
  32.2 6.9 %collective-permute-done.1 = bf16[3,2048,128]{2,1,0:T(8,128)(2,1)} collective-permute-done((bf16[3,2048,128]{2,1,0:T(8,128)(2,1)}, bf16[3,2048,128]{2,1,0:T(8,128)(2,1)}, u32[]{:S(2)}, u32[]{:S(2)}) %collective-permute-start.1) | collective-permute-done | bytes 1572896 | tf_op jit(solution)/shard_map/ppermute | solution.py:42
  39.2 3.5 %collective-permute-done.3 = bf16[3,2048,128]{2,1,0:T(8,128)(2,1)} collective-permute-done((bf16[3,2048,128]{2,1,0:T(8,128)(2,1)}, bf16[3,2048,128]{2,1,0:T(8,128)(2,1)}, u32[]{:S(2)}, u32[]{:S(2)}) %collective-permute-start.3) | collective-permute-done | bytes 1572896 | tf_op jit(solution)/shard_map/ppermute | solution.py:42
  42.7 2.7 %broadcast_select_fusion = bf16[3,2048,128]{2,1,0:T(8,128)(2,1)} fusion(bf16[3,2048,128]{2,1,0:T(8,128)(2,1)} %collective-permute-done.3, bf16[3,2048,128]{2,1,0:T(8,128)(2,1)} %collective-permute-done.1, pred[]{:T(512)S(6)} %eq.60), kind=kLoop, calls=%fused_computation | loop fusion | flops 786432 | bytes 4718593 | tf_op jit(solution)/shard_map/jit(_where)/select_n | solution.py:374
  45.4 0.0 copy-start.1
  45.4 7.1 %collective-permute-start.5 = (bf16[3,2048,128]{2,1,0:T(8,128)(2,1)}, bf16[3,2048,128]{2,1,0:T(8,128)(2,1)}, u32[]{:S(2)}, u32[]{:S(2)}) collective-permute-start(bf16[3,2048,128]{2,1,0:T(8,128)(2,1)} %broadcast_select_fusion), channel_id=1, source_target_pairs={{0,384},{64,192},{128,0},{192,320},{256,128},{320,448},{384,256},{... | collective-permute-start | bytes 4718600 | tf_op jit(solution)/shard_map/ppermute | solution.py:42
  52.5 0.0 all-to-all-done
  52.5 0.0 collective-permute-done
  52.6 0.0 copy-start.3
  52.6 0.0 copy-done
  52.6 0.9 shard_map.137
  53.5 14.6 %all_to_all.40.arrived = f32[8,16,256]{2,1,0:T(8,128)S(1)} all-to-all(f32[8,16,256]{2,1,0:T(8,128)S(1)} %get-tuple-element.30), channel_id=1, replica_groups=mesh['dp'=8,'expert_0'=8,'expert_1'=8] {'expert_0'}, dimensions={0} | all-to-all | bytes 262144 | tf_op jit(solution)/shard_map/all_to_all | solution.py:46
  68.1 17.8 %all_to_all.41.arrived = f32[8,16,256]{2,1,0:T(8,128)S(1)} all-to-all(f32[8,16,256]{2,1,0:T(8,128)S(1)} %shard_map.138), channel_id=1, replica_groups=mesh['dp'=8,'expert_0'=8,'expert_1'=8] {'expert_1'}, dimensions={0} | all-to-all | bytes 262144 | tf_op jit(solution)/shard_map/all_to_all | solution.py:46
  85.8 0.0 copy-done.2
  85.8 0.0 copy-done.1
  85.8 0.0 copy-start.4
  85.8 1.8 shard_map.139
  87.6 0.0 copy-done.3
  87.6 0.0 copy-start.6
  87.6 0.0 copy-start.5
  87.6 0.0 copy-start.7
  87.6 4.8 %all-to-all-start.3 = ((bf16[64,32,256]{2,1,0:T(8,128)(2,1)}), bf16[64,32,256]{2,1,0:T(8,128)(2,1)S(1)}, u32[]{:S(2)}, u32[]{:S(2)}) async-start(bf16[64,32,256]{2,1,0:T(8,128)(2,1)} %shard_map.139), calls=%async_computation.3 | async-start | bytes 2097152 | tf_op jit(solution)/shard_map/all_to_all | solution.py:46
  92.4 8.3 %collective-permute-start.2 = (bf16[3,2048,128]{2,1,0:T(8,128)(2,1)}, bf16[3,2048,128]{2,1,0:T(8,128)(2,1)}, u32[]{:S(2)}, u32[]{:S(2)}) collective-permute-start(bf16[3,2048,128]{2,1,0:T(8,128)(2,1)} %collective-permute-done.1), channel_id=1, source_target_pairs={{0,64},{64,0},{128,192},{192,128},{256,320},{320,256},{384,448},{4... | collective-permute-start | bytes 4718600 | tf_op jit(solution)/shard_map/ppermute | solution.py:42
  100.8 1.9 %collective-permute-start.4 = (bf16[3,2048,128]{2,1,0:T(8,128)(2,1)}, bf16[3,2048,128]{2,1,0:T(8,128)(2,1)}, u32[]{:S(2)}, u32[]{:S(2)}) collective-permute-start(bf16[3,2048,128]{2,1,0:T(8,128)(2,1)} %collective-permute-done.3), channel_id=1, source_target_pairs={{0,64},{64,0},{128,192},{192,128},{256,320},{320,256},{384,448},{4... | collective-permute-start | bytes 4718600 | tf_op jit(solution)/shard_map/ppermute | solution.py:42
  102.7 0.0 copy-done.4
  102.7 0.1 copy.31
  102.8 0.1 eq.50
  103.0 0.6 reduce-window.6
  103.6 0.2 slice_reduce_fusion
  103.8 0.0 collective-permute-done.5
  103.8 2.4 %collective-permute-start.6 = (bf16[3,2048,128]{2,1,0:T(8,128)(2,1)}, bf16[3,2048,128]{2,1,0:T(8,128)(2,1)}, u32[]{:S(2)}, u32[]{:S(2)}) collective-permute-start(bf16[3,2048,128]{2,1,0:T(8,128)(2,1)} %collective-permute-done.5), channel_id=1, source_target_pairs={{0,64},{64,0},{128,192},{192,128},{256,320},{320,256},{384,448},{4... | collective-permute-start | bytes 4718600 | tf_op jit(solution)/shard_map/ppermute | solution.py:42
  106.2 0.1 bitcast_bitcast_fusion
  106.3 0.1 eq.59
  106.5 0.1 copy.34
  106.6 0.1 fusion.1
  106.7 0.1 copy.35
  106.8 0.0 copy-done.6
  106.8 0.1 select_reduce_fusion
  107.0 0.1 copy.36
  107.0 0.0 copy-done.5
  107.1 0.0 copy-done.7
  107.1 0.8 shard_map.140
  108.0 0.0 collective-permute-done.2
  108.0 0.0 collective-permute-done.4
  108.0 6.9 %all-to-all-done.3.arrived = bf16[64,32,256]{2,1,0:T(8,128)(2,1)S(1)} async-done(((bf16[64,32,256]{2,1,0:T(8,128)(2,1)}), bf16[64,32,256]{2,1,0:T(8,128)(2,1)S(1)}, u32[]{:S(2)}, u32[]{:S(2)}) %all-to-all-start.3) | async-done | bytes 1048608 | tf_op jit(solution)/shard_map/all_to_all | solution.py:46
  114.9 0.5 shard_map.141
  115.3 17.5 %all_to_all.42 = bf16[8,32,256]{2,1,0:T(8,128)(2,1)S(1)} all-to-all(bf16[8,32,256]{2,1,0:T(8,128)(2,1)S(1)} %get-tuple-element.40), channel_id=1, replica_groups=mesh['dp'=8,'expert_0'=8,'expert_1'=8] {'dp'}, dimensions={0} | all-to-all | bytes 262144 | tf_op jit(solution)/shard_map/all_to_all | solution.py:46
  132.8 0.9 shard_map.142
  133.8 6.1 %all-to-all-start.5 = ((bf16[64,8,256]{2,1,0:T(8,128)(2,1)}), bf16[64,8,256]{2,1,0:T(8,128)(2,1)S(1)}, u32[]{:S(2)}, u32[]{:S(2)}) async-start(bf16[64,8,256]{2,1,0:T(8,128)(2,1)} %bitcast.50), calls=%async_computation.5 | async-start | bytes 524288 | tf_op jit(solution)/shard_map/all_to_all | solution.py:46
  139.9 0.0 collective-permute-done.6
  139.9 12.4 %all-to-all-done.5 = bf16[64,8,256]{2,1,0:T(8,128)(2,1)S(1)} async-done(((bf16[64,8,256]{2,1,0:T(8,128)(2,1)}), bf16[64,8,256]{2,1,0:T(8,128)(2,1)S(1)}, u32[]{:S(2)}, u32[]{:S(2)}) %all-to-all-start.5) | async-done | bytes 262176 | tf_op jit(solution)/shard_map/all_to_all | solution.py:46
  152.3 7.1 %shard_map.143 = bf16[512,256]{1,0:T(8,128)(2,1)S(1)} custom-call(bf16[512,256]{1,0:T(8,128)(2,1)S(1)} %bitcast.39, bf16[1,3,2048,128]{3,2,1,0:T(8,128)(2,1)} %bitcast.48, bf16[1,3,2048,128]{3,2,1,0:T(8,128)(2,1)} %bitcast.16.rest_1_, bf16[1,3,2048,128]{3,2,1,0:T(8,128)(2,1)} %bitcast.17.rest_2_, bf16[1,3,2048,128]{3,2,1,0:T(8,128)(2,1)} %bitcast.49, ...), custom_call_target="tpu_custom_call" | custom-call | flops 805306368 | bytes 12582912 | tf_op jit(solution)/shard_map/pallas_call | solution.py:307
  159.4 18.3 %all_to_all.43 = bf16[64,8,256]{2,1,0:T(8,128)(2,1)S(1)} all-to-all(bf16[64,8,256]{2,1,0:T(8,128)(2,1)S(1)} %bitcast.40), channel_id=1, replica_groups=mesh['dp'=8,'expert_0'=8,'expert_1'=8] {'expert_0','expert_1'}, dimensions={0} | all-to-all | bytes 524288 | tf_op jit(solution)/shard_map/all_to_all | solution.py:46
  177.7 0.4 shard_map.144
  178.1 11.1 %all_to_all.44.arrived = bf16[8,32,256]{2,1,0:T(8,128)(2,1)S(1)} all-to-all(bf16[8,32,256]{2,1,0:T(8,128)(2,1)S(1)} %bitcast.44), channel_id=1, replica_groups=mesh['dp'=8,'expert_0'=8,'expert_1'=8] {'dp'}, dimensions={0} | all-to-all | bytes 262144 | tf_op jit(solution)/shard_map/all_to_all | solution.py:46
  189.2 0.6 shard_map.145
  (13 shorter events, 0.2 us)
Async XLA Ops:
  5.4 33.8 %collective-permute-start.1 = (bf16[3,2048,128]{2,1,0:T(8,128)(2,1)}, bf16[3,2048,128]{2,1,0:T(8,128)(2,1)}, u32[]{:S(2)}, u32[]{:S(2)}) collective-permute-start(bf16[3,2048,128]{2,1,0:T(8,128)(2,1)} %get-tuple-element.28), channel_id=1, source_target_pairs={{0,128},{64,192},{128,256},{192,320},{256,384},{320,448},{384,0},{... | collective-permute-start | bytes 4718600 | tf_op jit(solution)/shard_map/ppermute | solution.py:42
  9.3 33.3 %collective-permute-start.3 = (bf16[3,2048,128]{2,1,0:T(8,128)(2,1)}, bf16[3,2048,128]{2,1,0:T(8,128)(2,1)}, u32[]{:S(2)}, u32[]{:S(2)}) collective-permute-start(bf16[3,2048,128]{2,1,0:T(8,128)(2,1)} %get-tuple-element.28), channel_id=1, source_target_pairs={{0,384},{64,448},{128,0},{192,64},{256,128},{320,192},{384,256},{4... | collective-permute-start | bytes 4718600 | tf_op jit(solution)/shard_map/ppermute | solution.py:42
  12.5 40.0 %collective-permute-start = (bf16[3,2048,128]{2,1,0:T(8,128)(2,1)}, bf16[3,2048,128]{2,1,0:T(8,128)(2,1)S(1)}, u32[]{:S(2)}, u32[]{:S(2)}) collective-permute-start(bf16[3,2048,128]{2,1,0:T(8,128)(2,1)} %get-tuple-element.28), channel_id=1, source_target_pairs={{0,64},{64,0},{128,192},{192,128},{256,320},{320,256},{384,448},{4... | collective-permute-start | bytes 4718600 | tf_op jit(solution)/shard_map/ppermute | solution.py:42
  21.2 31.3 %all-to-all-start = ((bf16[64,8,128]{2,1,0:T(8,128)(2,1)}), bf16[64,8,128]{2,1,0:T(8,128)(2,1)S(1)}, u32[]{:S(2)}, u32[]{:S(2)}) async-start(bf16[64,8,128]{2,1,0:T(8,128)(2,1)} %bitcast.54), calls=%async_computation | async-start | bytes 262144 | tf_op jit(solution)/shard_map/all_to_all | solution.py:46
  32.2 20.4 %copy-start = (bf16[128,2048]{1,0:T(8,128)(2,1)S(1)}, bf16[128,2048]{1,0:T(8,128)(2,1)}, u32[]{:S(2)}) copy-start(bf16[128,2048]{1,0:T(8,128)(2,1)} %down.1) | copy-start | bytes 1572868
  32.2 53.6 %copy-start.2 = (bf16[32,2048]{1,0:T(8,128)(2,1)S(1)}, bf16[32,2048]{1,0:T(8,128)(2,1)}, u32[]{:S(2)}) copy-start(bf16[32,2048]{1,0:T(8,128)(2,1)} %up.1) | copy-start | bytes 393220
  45.4 40.4 %copy-start.1 = (bf16[128,2048]{1,0:T(8,128)(2,1)S(1)}, bf16[128,2048]{1,0:T(8,128)(2,1)}, u32[]{:S(2)}) copy-start(bf16[128,2048]{1,0:T(8,128)(2,1)} %value.1) | copy-start | bytes 1572868
  45.4 58.4 %collective-permute-start.5 = (bf16[3,2048,128]{2,1,0:T(8,128)(2,1)}, bf16[3,2048,128]{2,1,0:T(8,128)(2,1)}, u32[]{:S(2)}, u32[]{:S(2)}) collective-permute-start(bf16[3,2048,128]{2,1,0:T(8,128)(2,1)} %broadcast_select_fusion), channel_id=1, source_target_pairs={{0,384},{64,192},{128,0},{192,320},{256,128},{320,448},{384,256},{... | collective-permute-start | bytes 4718600 | tf_op jit(solution)/shard_map/ppermute | solution.py:42
  52.6 35.1 %copy-start.3 = (bf16[3,2048,128]{2,1,0:T(8,128)(2,1)}, bf16[3,2048,128]{2,1,0:T(8,128)(2,1)S(1)}, u32[]{:S(2)}) copy-start(bf16[3,2048,128]{2,1,0:T(8,128)(2,1)S(1)} %collective-permute-done) | copy-start | bytes 4718596
  85.8 16.9 %copy-start.4 = (s32[32,6]{0,1:T(8,128)S(1)}, s32[32,6]{0,1:T(8,128)}, u32[]{:S(2)}) copy-start(s32[32,6]{0,1:T(8,128)} %param.23) | copy-start | bytes 2308
  87.6 19.2 %copy-start.6 = (f32[32,6]{0,1:T(8,128)S(1)}, f32[32,6]{0,1:T(8,128)}, u32[]{:S(2)}) copy-start(f32[32,6]{0,1:T(8,128)} %param.24) | copy-start | bytes 2308
  87.6 19.4 %copy-start.5 = (bf16[4,2048]{1,0:T(4,128)(2,1)S(1)}, bf16[4,2048]{1,0:T(4,128)(2,1)}, u32[]{:S(2)}) copy-start(bf16[4,2048]{1,0:T(4,128)(2,1)} %param.17) | copy-start | bytes 49156
  87.6 19.5 %copy-start.7 = (bf16[2048]{0:T(1024)(128)(2,1)S(1)}, bf16[2048]{0:T(1024)(128)(2,1)}, u32[]{:S(2)}) copy-start(bf16[2048]{0:T(1024)(128)(2,1)} %param.22) | copy-start | bytes 12292
  87.6 27.2 %all-to-all-start.3 = ((bf16[64,32,256]{2,1,0:T(8,128)(2,1)}), bf16[64,32,256]{2,1,0:T(8,128)(2,1)S(1)}, u32[]{:S(2)}, u32[]{:S(2)}) async-start(bf16[64,32,256]{2,1,0:T(8,128)(2,1)} %shard_map.139), calls=%async_computation.3 | async-start | bytes 2097152 | tf_op jit(solution)/shard_map/all_to_all | solution.py:46
  92.4 15.5 %collective-permute-start.2 = (bf16[3,2048,128]{2,1,0:T(8,128)(2,1)}, bf16[3,2048,128]{2,1,0:T(8,128)(2,1)}, u32[]{:S(2)}, u32[]{:S(2)}) collective-permute-start(bf16[3,2048,128]{2,1,0:T(8,128)(2,1)} %collective-permute-done.1), channel_id=1, source_target_pairs={{0,64},{64,0},{128,192},{192,128},{256,320},{320,256},{384,448},{4... | collective-permute-start | bytes 4718600 | tf_op jit(solution)/shard_map/ppermute | solution.py:42
  100.8 7.2 %collective-permute-start.4 = (bf16[3,2048,128]{2,1,0:T(8,128)(2,1)}, bf16[3,2048,128]{2,1,0:T(8,128)(2,1)}, u32[]{:S(2)}, u32[]{:S(2)}) collective-permute-start(bf16[3,2048,128]{2,1,0:T(8,128)(2,1)} %collective-permute-done.3), channel_id=1, source_target_pairs={{0,64},{64,0},{128,192},{192,128},{256,320},{320,256},{384,448},{4... | collective-permute-start | bytes 4718600 | tf_op jit(solution)/shard_map/ppermute | solution.py:42
  103.8 36.1 %collective-permute-start.6 = (bf16[3,2048,128]{2,1,0:T(8,128)(2,1)}, bf16[3,2048,128]{2,1,0:T(8,128)(2,1)}, u32[]{:S(2)}, u32[]{:S(2)}) collective-permute-start(bf16[3,2048,128]{2,1,0:T(8,128)(2,1)} %collective-permute-done.5), channel_id=1, source_target_pairs={{0,64},{64,0},{128,192},{192,128},{256,320},{320,256},{384,448},{4... | collective-permute-start | bytes 4718600 | tf_op jit(solution)/shard_map/ppermute | solution.py:42
  133.8 18.5 %all-to-all-start.5 = ((bf16[64,8,256]{2,1,0:T(8,128)(2,1)}), bf16[64,8,256]{2,1,0:T(8,128)(2,1)S(1)}, u32[]{:S(2)}, u32[]{:S(2)}) async-start(bf16[64,8,256]{2,1,0:T(8,128)(2,1)} %bitcast.50), calls=%async_computation.5 | async-start | bytes 524288 | tf_op jit(solution)/shard_map/all_to_all | solution.py:46

commit v6 on v5

--- a/solution.py
+++ b/solution.py
@@ -316,7 +316,7 @@
             bytes_accessed=6 * width * hidden,
             transcendentals=0,
         ),
-        compiler_params=pltpu.CompilerParams(vmem_limit_bytes=52 * 2**20),
+        compiler_params=pltpu.CompilerParams(vmem_limit_bytes=51 * 2**20),
     )(rows, *weights)
 
 
@@ -369,8 +369,6 @@
     from_above = moved(joined, downs)
     shards = [joined, from_below, from_above]
     own_swapped = moved(joined, swap)
-    arrived, own_swapped = lax.optimization_barrier((arrived, own_swapped))
-    shards.append(own_swapped)
     on = jnp.where(lax.axis_index("dp") % 2 == 0, from_above, from_below)
     relayed = [downs[d] if d % 2 == 0 else ups[d] for d in range(dp_count)]
     opposite = moved(on, relayed)
@@ -420,12 +418,11 @@
     gain_cut = jnp.broadcast_to(
         cut_rows(norm_gain.astype(F32)), (CUTS, requests, columns)
     ).reshape(CUTS * requests, columns)
-    at_home, pick, give, residual_cut, gain_cut, below_swapped, above_swapped = (
-        lax.optimization_barrier(
-            (at_home, pick, give, residual_cut, gain_cut, below_swapped, above_swapped)
-        )
-    )
-    shards += [opposite, below_swapped, above_swapped, opposite_swapped]
+    swapped = (own_swapped, below_swapped, above_swapped)
+    at_home, pick, give, residual_cut, gain_cut, *swapped = lax.optimization_barrier(
+        (at_home, pick, give, residual_cut, gain_cut, *swapped)
+    )
+    shards += [opposite, *swapped, opposite_swapped]
     stream, copies = call(
         norm_kernel,
         (shape((CUTS * requests, columns), F32), shape((dp_count, CUTS * requests, columns), BF16)),

time: 191 us -> 190 us (level)
  blocking collectives: 79.2 us -> 99.7 us
  waiting for transfers between devices: 29.7 us -> 14.5 us
  starting transfers between devices: 57.4 us -> 51.5 us
    all_to_all x5 -> x6, blocking collectives: 79.2 us -> 99.7 us  [exchange(): return lax.all_to_all(rows, axis, split_axis=0, concat_axis=0, tiled=True)]
    all_to_all x3 -> x2, waiting for transfers between devices: 19.3 us -> 0.87 us  [exchange(): return lax.all_to_all(rows, axis, split_axis=0, concat_axis=0, tiled=True)]
    ppermute x7, starting transfers between devices: 35.6 us -> 30.2 us  [moved(): return lax.ppermute(block, 'dp', list(enumerate(where)))]
    ppermute x7, waiting for transfers between devices: 10.4 us -> 13.6 us  [moved(): return lax.ppermute(block, 'dp', list(enumerate(where)))]
    all_to_all x3 -> x2, starting transfers between devices: 21.9 us -> 21.3 us  [exchange(): return lax.all_to_all(rows, axis, split_axis=0, concat_axis=0, tiled=True)]
  transfers between devices with their start and end apart: 10 -> 9, of which waited for: 4 -> 3; matrix products, arithmetic and copies ran while one was open for 2% -> 2% of each run, Pallas kernels for 3% -> 3%
where the time goes in v6:
time: 190 us; the launch traced here: 189 us
  blocking collectives  99.7 us (52%)
  starting transfers between devices  51.5 us (27%)
  Pallas kernels  18.3 us (10%)
  waiting for transfers between devices  14.5 us (8%)
  local copies, waits for them, and re-layouts  2.47 us (1%)
  other arithmetic  2.41 us (1%)
    all_to_all x6, blocking collectives, exchange(): return lax.all_to_all(rows, axis, split_axis=0, concat_axis=0, tiled=True)  99.7 us
    ppermute x7, starting transfers between devices, moved(): return lax.ppermute(block, 'dp', list(enumerate(where)))  30.2 us
    all_to_all x2, starting transfers between devices, exchange(): return lax.all_to_all(rows, axis, split_axis=0, concat_axis=0, tiled=True)  21.3 us
    ppermute x7, waiting for transfers between devices, moved(): return lax.ppermute(block, 'dp', list(enumerate(where)))  13.6 us
    pallas_call x1, Pallas kernels, ffn(): pl.pallas_call(ffn_kernel, out_shape=shape(rows.shape, BF16), in_specs=[W...  6.91 us
    pallas_call x1, Pallas kernels, attend(): pl.pallas_call(attend_kernel, out_shape=(shape((owners * 2 * n, lanes), B...  5.41 us
  transfers between devices with their start and end apart: 9, of which 3 were waited for; matrix products, arithmetic and copies ran while one was open for 2% of the time, Pallas kernels for 3%

profile of v6, /device:TPU:1, one launch (start us, length us, event | category | flops | bytes accessed | tf_op | source)
XLA Modules:
  0.0 189.2 jit_solution(2033038093992392467)
XLA Ops:
  0.0 5.4 %shard_map.136 = (bf16[512,128]{1,0:T(8,128)(2,1)}, bf16[3,2048,128]{2,1,0:T(8,128)(2,1)}) custom-call(s32[4]{0:T(128)} %lengths.1, s32[4]{0:T(128)} %ids.1, bf16[4,16,576]{2,1,0:T(8,128)(2,1)} %query.1, bf16[4,576,512]{2,1,0:T(8,128)(2,1)} %bitcast.49, bf16[2048,128]{1,0:T(8,128)(2,1)} %bitcast.51, bf16[2048,128]{1,0:T(8,128)(2,1)} %bitcast.52, ...), custom_call_target="tpu_custom_call" | custom-call | flops 75497472 | bytes 2359296 | tf_op jit(solution)/shard_map/pallas_call | solution.py:125
  5.4 3.9 %collective-permute-start.1 = (bf16[3,2048,128]{2,1,0:T(8,128)(2,1)}, bf16[3,2048,128]{2,1,0:T(8,128)(2,1)S(1)}, u32[]{:S(2)}, u32[]{:S(2)}) collective-permute-start(bf16[3,2048,128]{2,1,0:T(8,128)(2,1)} %get-tuple-element.32), channel_id=1, source_target_pairs={{0,128},{64,192},{128,256},{192,320},{256,384},{320,448},{384,0},{... | collective-permute-start | bytes 4718600 | tf_op jit(solution)/shard_map/ppermute | solution.py:42
  9.4 3.2 %collective-permute-start.3 = (bf16[3,2048,128]{2,1,0:T(8,128)(2,1)}, bf16[3,2048,128]{2,1,0:T(8,128)(2,1)}, u32[]{:S(2)}, u32[]{:S(2)}) collective-permute-start(bf16[3,2048,128]{2,1,0:T(8,128)(2,1)} %get-tuple-element.32), channel_id=1, source_target_pairs={{0,384},{64,448},{128,0},{192,64},{256,128},{320,192},{384,256},{4... | collective-permute-start | bytes 4718600 | tf_op jit(solution)/shard_map/ppermute | solution.py:42
  12.6 16.5 %all-to-all-start = ((bf16[64,8,128]{2,1,0:T(8,128)(2,1)}), bf16[64,8,128]{2,1,0:T(8,128)(2,1)S(1)}, u32[]{:S(2)}, u32[]{:S(2)}) async-start(bf16[64,8,128]{2,1,0:T(8,128)(2,1)} %bitcast.54), calls=%async_computation | async-start | bytes 262144 | tf_op jit(solution)/shard_map/all_to_all | solution.py:46
  29.1 0.0 copy-start.1
  29.1 0.0 copy-start.5
  29.1 10.0 %collective-permute-done.1 = bf16[3,2048,128]{2,1,0:T(8,128)(2,1)S(1)} collective-permute-done((bf16[3,2048,128]{2,1,0:T(8,128)(2,1)}, bf16[3,2048,128]{2,1,0:T(8,128)(2,1)S(1)}, u32[]{:S(2)}, u32[]{:S(2)}) %collective-permute-start.1) | collective-permute-done | bytes 1572896 | tf_op jit(solution)/shard_map/ppermute | solution.py:42
  39.1 0.0 copy-start.6
  39.1 3.6 %collective-permute-done.3 = bf16[3,2048,128]{2,1,0:T(8,128)(2,1)} collective-permute-done((bf16[3,2048,128]{2,1,0:T(8,128)(2,1)}, bf16[3,2048,128]{2,1,0:T(8,128)(2,1)}, u32[]{:S(2)}, u32[]{:S(2)}) %collective-permute-start.3) | collective-permute-done | bytes 1572896 | tf_op jit(solution)/shard_map/ppermute | solution.py:42
  42.7 0.0 copy-done.6
  42.7 1.3 broadcast_select_fusion
  44.0 0.0 copy-start.2
  44.0 7.1 %collective-permute-start.5 = (bf16[3,2048,128]{2,1,0:T(8,128)(2,1)}, bf16[3,2048,128]{2,1,0:T(8,128)(2,1)}, u32[]{:S(2)}, u32[]{:S(2)}) collective-permute-start(bf16[3,2048,128]{2,1,0:T(8,128)(2,1)} %broadcast_select_fusion), channel_id=1, source_target_pairs={{0,384},{64,192},{128,0},{192,320},{256,128},{320,448},{384,256},{... | collective-permute-start | bytes 4718600 | tf_op jit(solution)/shard_map/ppermute | solution.py:42
  51.2 0.0 all-to-all-done
  51.2 0.0 copy-done.1
  51.2 0.9 shard_map.137
  52.1 14.6 %all_to_all.40.arrived = f32[8,16,256]{2,1,0:T(8,128)S(1)} all-to-all(f32[8,16,256]{2,1,0:T(8,128)S(1)} %get-tuple-element.27), channel_id=1, replica_groups=mesh['dp'=8,'expert_0'=8,'expert_1'=8] {'expert_0'}, dimensions={0} | all-to-all | bytes 262144 | tf_op jit(solution)/shard_map/all_to_all | solution.py:46
  66.7 17.8 %all_to_all.41.arrived = f32[8,16,256]{2,1,0:T(8,128)S(1)} all-to-all(f32[8,16,256]{2,1,0:T(8,128)S(1)} %shard_map.138), channel_id=1, replica_groups=mesh['dp'=8,'expert_0'=8,'expert_1'=8] {'expert_1'}, dimensions={0} | all-to-all | bytes 262144 | tf_op jit(solution)/shard_map/all_to_all | solution.py:46
  84.4 0.0 copy-done.5
  84.4 0.0 copy-done.2
  84.4 0.0 copy-start
  84.4 0.0 copy-start.7
  84.4 1.7 shard_map.139
  86.2 0.0 copy-start.8
  86.2 4.8 %all-to-all-start.3 = ((bf16[64,32,256]{2,1,0:T(8,128)(2,1)}), bf16[64,32,256]{2,1,0:T(8,128)(2,1)S(1)}, u32[]{:S(2)}, u32[]{:S(2)}) async-start(bf16[64,32,256]{2,1,0:T(8,128)(2,1)} %shard_map.139), calls=%async_computation.3 | async-start | bytes 2097152 | tf_op jit(solution)/shard_map/all_to_all | solution.py:46
  91.0 0.0 copy-done
  91.0 9.7 %collective-permute-start = (bf16[3,2048,128]{2,1,0:T(8,128)(2,1)S(1)}, bf16[3,2048,128]{2,1,0:T(8,128)(2,1)}, u32[]{:S(2)}, u32[]{:S(2)}) collective-permute-start(bf16[3,2048,128]{2,1,0:T(8,128)(2,1)S(1)} %copy-done), channel_id=1, source_target_pairs={{0,64},{64,0},{128,192},{192,128},{256,320},{320,256},{384,448},{4... | collective-permute-start | bytes 4718600 | tf_op jit(solution)/shard_map/ppermute | solution.py:42
  100.7 1.9 %collective-permute-start.2 = (bf16[3,2048,128]{2,1,0:T(8,128)(2,1)}, bf16[3,2048,128]{2,1,0:T(8,128)(2,1)}, u32[]{:S(2)}, u32[]{:S(2)}) collective-permute-start(bf16[3,2048,128]{2,1,0:T(8,128)(2,1)} %copy-done.6), channel_id=1, source_target_pairs={{0,64},{64,0},{128,192},{192,128},{256,320},{320,256},{384,448},{4... | collective-permute-start | bytes 4718600 | tf_op jit(solution)/shard_map/ppermute | solution.py:42
  102.7 2.4 %collective-permute-start.4 = (bf16[3,2048,128]{2,1,0:T(8,128)(2,1)}, bf16[3,2048,128]{2,1,0:T(8,128)(2,1)}, u32[]{:S(2)}, u32[]{:S(2)}) collective-permute-start(bf16[3,2048,128]{2,1,0:T(8,128)(2,1)} %collective-permute-done.3), channel_id=1, source_target_pairs={{0,64},{64,0},{128,192},{192,128},{256,320},{320,256},{384,448},{4... | collective-permute-start | bytes 4718600 | tf_op jit(solution)/shard_map/ppermute | solution.py:42
  105.1 0.0 copy-done.7
  105.1 0.1 copy.31
  105.2 0.1 eq.50
  105.3 0.6 reduce-window.6
  105.9 0.2 slice_reduce_fusion
  106.2 0.0 collective-permute-done.5
  106.2 1.9 %collective-permute-start.6 = (bf16[3,2048,128]{2,1,0:T(8,128)(2,1)}, bf16[3,2048,128]{2,1,0:T(8,128)(2,1)}, u32[]{:S(2)}, u32[]{:S(2)}) collective-permute-start(bf16[3,2048,128]{2,1,0:T(8,128)(2,1)} %collective-permute-done.5), channel_id=1, source_target_pairs={{0,64},{64,0},{128,192},{192,128},{256,320},{320,256},{384,448},{4... | collective-permute-start | bytes 4718600 | tf_op jit(solution)/shard_map/ppermute | solution.py:42
  108.1 0.1 bitcast_bitcast_fusion
  108.2 0.1 eq.59
  108.3 0.1 copy.34
  108.4 0.1 fusion.1
  108.6 0.1 copy.35
  108.7 0.0 copy-done.9
  108.7 0.1 select_reduce_fusion
  108.8 0.1 copy.36
  108.9 0.0 copy-done.8
  109.0 0.0 copy-done.10
  109.0 0.8 shard_map.140
  109.9 0.0 copy-start.3
  109.9 0.7 copy-done.3
  110.6 0.0 collective-permute-done
  110.6 0.9 all-to-all-done.3.arrived
  111.4 0.0 collective-permute-done.2
  111.4 0.0 collective-permute-done.4
  111.4 0.5 shard_map.141
  111.9 19.4 %all_to_all.42 = bf16[8,32,256]{2,1,0:T(8,128)(2,1)S(1)} all-to-all(bf16[8,32,256]{2,1,0:T(8,128)(2,1)S(1)} %get-tuple-element.38), channel_id=1, replica_groups=mesh['dp'=8,'expert_0'=8,'expert_1'=8] {'dp'}, dimensions={0} | all-to-all | bytes 262144 | tf_op jit(solution)/shard_map/all_to_all | solution.py:46
  131.3 0.9 copy-done.4
  132.3 0.9 shard_map.142
  133.2 18.6 %all_to_all.43 = bf16[64,8,256]{2,1,0:T(8,128)(2,1)S(1)} all-to-all(bf16[64,8,256]{2,1,0:T(8,128)(2,1)} %bitcast.50), channel_id=1, replica_groups=mesh['dp'=8,'expert_0'=8,'expert_1'=8] {'expert_0','expert_1'}, dimensions={0} | all-to-all | bytes 524288 | tf_op jit(solution)/shard_map/all_to_all | solution.py:46
  151.8 0.0 collective-permute-done.6
  151.8 6.9 %shard_map.143 = bf16[512,256]{1,0:T(8,128)(2,1)S(1)} custom-call(bf16[512,256]{1,0:T(8,128)(2,1)S(1)} %bitcast.40, bf16[1,3,2048,128]{3,2,1,0:T(8,128)(2,1)S(1)} %bitcast.39, bf16[1,3,2048,128]{3,2,1,0:T(8,128)(2,1)} %bitcast.48, bf16[1,3,2048,128]{3,2,1,0:T(8,128)(2,1)} %bitcast.17.rest_2_, bf16[1,3,2048,128]{3,2,1,0:T(8,128)(2,1)} %bitcast.18.rest_3_, ...), custom_call_target="tpu_custom_call" | custom-call | flops 805306368 | bytes 12582912 | tf_op jit(solution)/shard_map/pallas_call | solution.py:307
  158.7 18.3 %all_to_all.44 = bf16[64,8,256]{2,1,0:T(8,128)(2,1)S(1)} all-to-all(bf16[64,8,256]{2,1,0:T(8,128)(2,1)S(1)} %bitcast.41), channel_id=1, replica_groups=mesh['dp'=8,'expert_0'=8,'expert_1'=8] {'expert_0','expert_1'}, dimensions={0} | all-to-all | bytes 524288 | tf_op jit(solution)/shard_map/all_to_all | solution.py:46
  177.0 0.4 shard_map.144
  177.4 11.1 %all_to_all.45.arrived = bf16[8,32,256]{2,1,0:T(8,128)(2,1)S(1)} all-to-all(bf16[8,32,256]{2,1,0:T(8,128)(2,1)S(1)} %bitcast.45), channel_id=1, replica_groups=mesh['dp'=8,'expert_0'=8,'expert_1'=8] {'dp'}, dimensions={0} | all-to-all | bytes 262144 | tf_op jit(solution)/shard_map/all_to_all | solution.py:46
  188.5 0.6 shard_map.145
  (16 shorter events, 0.2 us)
Async XLA Ops:
  5.4 33.7 %collective-permute-start.1 = (bf16[3,2048,128]{2,1,0:T(8,128)(2,1)}, bf16[3,2048,128]{2,1,0:T(8,128)(2,1)S(1)}, u32[]{:S(2)}, u32[]{:S(2)}) collective-permute-start(bf16[3,2048,128]{2,1,0:T(8,128)(2,1)} %get-tuple-element.32), channel_id=1, source_target_pairs={{0,128},{64,192},{128,256},{192,320},{256,384},{320,448},{384,0},{... | collective-permute-start | bytes 4718600 | tf_op jit(solution)/shard_map/ppermute | solution.py:42
  9.4 33.3 %collective-permute-start.3 = (bf16[3,2048,128]{2,1,0:T(8,128)(2,1)}, bf16[3,2048,128]{2,1,0:T(8,128)(2,1)}, u32[]{:S(2)}, u32[]{:S(2)}) collective-permute-start(bf16[3,2048,128]{2,1,0:T(8,128)(2,1)} %get-tuple-element.32), channel_id=1, source_target_pairs={{0,384},{64,448},{128,0},{192,64},{256,128},{320,192},{384,256},{4... | collective-permute-start | bytes 4718600 | tf_op jit(solution)/shard_map/ppermute | solution.py:42
  12.6 38.6 %all-to-all-start = ((bf16[64,8,128]{2,1,0:T(8,128)(2,1)}), bf16[64,8,128]{2,1,0:T(8,128)(2,1)S(1)}, u32[]{:S(2)}, u32[]{:S(2)}) async-start(bf16[64,8,128]{2,1,0:T(8,128)(2,1)} %bitcast.54), calls=%async_computation | async-start | bytes 262144 | tf_op jit(solution)/shard_map/all_to_all | solution.py:46
  29.1 22.1 %copy-start.1 = (bf16[128,2048]{1,0:T(8,128)(2,1)S(1)}, bf16[128,2048]{1,0:T(8,128)(2,1)}, u32[]{:S(2)}) copy-start(bf16[128,2048]{1,0:T(8,128)(2,1)} %down.1) | copy-start | bytes 1572868
  29.1 55.3 %copy-start.5 = (bf16[32,2048]{1,0:T(8,128)(2,1)S(1)}, bf16[32,2048]{1,0:T(8,128)(2,1)}, u32[]{:S(2)}) copy-start(bf16[32,2048]{1,0:T(8,128)(2,1)} %up.1) | copy-start | bytes 393220
  39.1 3.6 %copy-start.6 = (bf16[3,2048,128]{2,1,0:T(8,128)(2,1)}, bf16[3,2048,128]{2,1,0:T(8,128)(2,1)S(1)}, u32[]{:S(2)}) copy-start(bf16[3,2048,128]{2,1,0:T(8,128)(2,1)S(1)} %collective-permute-done.1) | copy-start | bytes 4718596
  44.0 40.4 %copy-start.2 = (bf16[128,2048]{1,0:T(8,128)(2,1)S(1)}, bf16[128,2048]{1,0:T(8,128)(2,1)}, u32[]{:S(2)}) copy-start(bf16[128,2048]{1,0:T(8,128)(2,1)} %value.1) | copy-start | bytes 1572868
  44.0 62.1 %collective-permute-start.5 = (bf16[3,2048,128]{2,1,0:T(8,128)(2,1)}, bf16[3,2048,128]{2,1,0:T(8,128)(2,1)}, u32[]{:S(2)}, u32[]{:S(2)}) collective-permute-start(bf16[3,2048,128]{2,1,0:T(8,128)(2,1)} %broadcast_select_fusion), channel_id=1, source_target_pairs={{0,384},{64,192},{128,0},{192,320},{256,128},{320,448},{384,256},{... | collective-permute-start | bytes 4718600 | tf_op jit(solution)/shard_map/ppermute | solution.py:42
  84.4 6.6 %copy-start = (bf16[3,2048,128]{2,1,0:T(8,128)(2,1)S(1)}, bf16[3,2048,128]{2,1,0:T(8,128)(2,1)}, u32[]{:S(2)}) copy-start(bf16[3,2048,128]{2,1,0:T(8,128)(2,1)} %get-tuple-element.32) | copy-start | bytes 4718596
  84.4 20.6 %copy-start.7 = (s32[32,6]{0,1:T(8,128)S(1)}, s32[32,6]{0,1:T(8,128)}, u32[]{:S(2)}) copy-start(s32[32,6]{0,1:T(8,128)} %param.23) | copy-start | bytes 2308
  86.2 22.5 %copy-start.9 = (f32[32,6]{0,1:T(8,128)S(1)}, f32[32,6]{0,1:T(8,128)}, u32[]{:S(2)}) copy-start(f32[32,6]{0,1:T(8,128)} %param.24) | copy-start | bytes 2308
  86.2 22.7 %copy-start.8 = (bf16[4,2048]{1,0:T(4,128)(2,1)S(1)}, bf16[4,2048]{1,0:T(4,128)(2,1)}, u32[]{:S(2)}) copy-start(bf16[4,2048]{1,0:T(4,128)(2,1)} %param.17) | copy-start | bytes 49156
  86.2 22.8 %copy-start.10 = (bf16[2048]{0:T(1024)(128)(2,1)S(1)}, bf16[2048]{0:T(1024)(128)(2,1)}, u32[]{:S(2)}) copy-start(bf16[2048]{0:T(1024)(128)(2,1)} %param.22) | copy-start | bytes 12292
  86.2 25.2 %all-to-all-start.3 = ((bf16[64,32,256]{2,1,0:T(8,128)(2,1)}), bf16[64,32,256]{2,1,0:T(8,128)(2,1)S(1)}, u32[]{:S(2)}, u32[]{:S(2)}) async-start(bf16[64,32,256]{2,1,0:T(8,128)(2,1)} %shard_map.139), calls=%async_computation.3 | async-start | bytes 2097152 | tf_op jit(solution)/shard_map/all_to_all | solution.py:46
  91.0 19.6 %collective-permute-start = (bf16[3,2048,128]{2,1,0:T(8,128)(2,1)S(1)}, bf16[3,2048,128]{2,1,0:T(8,128)(2,1)}, u32[]{:S(2)}, u32[]{:S(2)}) collective-permute-start(bf16[3,2048,128]{2,1,0:T(8,128)(2,1)S(1)} %copy-done), channel_id=1, source_target_pairs={{0,64},{64,0},{128,192},{192,128},{256,320},{320,256},{384,448},{4... | collective-permute-start | bytes 4718600 | tf_op jit(solution)/shard_map/ppermute | solution.py:42
  100.7 10.7 %collective-permute-start.2 = (bf16[3,2048,128]{2,1,0:T(8,128)(2,1)}, bf16[3,2048,128]{2,1,0:T(8,128)(2,1)}, u32[]{:S(2)}, u32[]{:S(2)}) collective-permute-start(bf16[3,2048,128]{2,1,0:T(8,128)(2,1)} %copy-done.6), channel_id=1, source_target_pairs={{0,64},{64,0},{128,192},{192,128},{256,320},{320,256},{384,448},{4... | collective-permute-start | bytes 4718600 | tf_op jit(solution)/shard_map/ppermute | solution.py:42
  102.7 8.8 %collective-permute-start.4 = (bf16[3,2048,128]{2,1,0:T(8,128)(2,1)}, bf16[3,2048,128]{2,1,0:T(8,128)(2,1)}, u32[]{:S(2)}, u32[]{:S(2)}) collective-permute-start(bf16[3,2048,128]{2,1,0:T(8,128)(2,1)} %collective-permute-done.3), channel_id=1, source_target_pairs={{0,64},{64,0},{128,192},{192,128},{256,320},{320,256},{384,448},{4... | collective-permute-start | bytes 4718600 | tf_op jit(solution)/shard_map/ppermute | solution.py:42
  106.2 45.6 %collective-permute-start.6 = (bf16[3,2048,128]{2,1,0:T(8,128)(2,1)}, bf16[3,2048,128]{2,1,0:T(8,128)(2,1)}, u32[]{:S(2)}, u32[]{:S(2)}) collective-permute-start(bf16[3,2048,128]{2,1,0:T(8,128)(2,1)} %collective-permute-done.5), channel_id=1, source_target_pairs={{0,64},{64,0},{128,192},{192,128},{256,320},{320,256},{384,448},{4... | collective-permute-start | bytes 4718600 | tf_op jit(solution)/shard_map/ppermute | solution.py:42
  109.9 0.7 copy-start.3
  131.3 1.0 copy-start.4
